TPU v7x, 32 devices: a whole 2x2x4 slice. The times are simulated.
32 devices in a mesh: srow: 4 (over y, core), scol: 8 (over z, x).
Axes of the slice: x: 2, y: 2, z: 4, core: 2. Of those that a mesh axis runs over, the one named last changes fastest.
Arguments:
- loads: float32 [4, 16, 4, 128], P('srow', 'scol'), may hold values from -6 to 6
- local_inverse: float32 [4, 16, 128, 128], P('srow', 'scol'), as said below
- dirichlet: float32 [4, 16, 128, 128], P('srow', 'scol'), as said below
- corner_coupling: float32 [4, 16, 128], P('srow', 'scol'), may hold values from -4 to 4
- coarse_inverse: float32 [4, 16, 16], P('srow', 'scol'), as said below
- partner: int32 [4, 16, 128], P('srow', 'scol'), may hold values from -1 to 31, as said below
Outputs:
- multipliers: float32 [4, 16, 4, 128], P('srow', 'scol')
- residual: float32 [4, 16, 4, 128], P('srow', 'scol')
Inputs may be any that keep to these rules, and one draw needn't show every extreme that they name: `partner`: on each edge of each subdomain the first n entries, for some n of 1 to 32, are the positions 0 to n - 1 in order or reversed, the rest are -1; the two subdomains sharing an edge have the same n and mutually inverse lists. `local_inverse`: each block is symmetric positive definite. `dirichlet`: each block is symmetric positive definite. `coarse_inverse`: each band's matrix is symmetric positive definite.
All inputs are finite; a program needn't handle non-finite values.
Results may differ from a plain program's by a relative error of at most 0.0003.
Values sent between devices are 32-bit elements; how exact they have to be, the bound alone decides.
A program may use at most 64 MiB of HBM per device.

v0:
```python
import jax
import jax.numpy as jnp
from jax import lax
from jax.sharding import PartitionSpec as P

ITERS = 3
precise = lax.Precision.HIGHEST


def with_halo(cells, sides, width):
    for axis, dim in sides:
        count = lax.axis_size(axis)
        head = lax.slice_in_dim(cells, 0, width, axis=dim)
        tail = lax.slice_in_dim(cells, cells.shape[dim] - width, cells.shape[dim], axis=dim)
        cells = jnp.concatenate(
            [
                lax.ppermute(tail, axis, [(i, (i + 1) % count) for i in range(count)]),
                cells,
                lax.ppermute(head, axis, [((i + 1) % count, i) for i in range(count)]),
            ],
            axis=dim,
        )
    return cells


def facing_edges(values):
    edge_len = values.shape[-1] // 4
    sideways = with_halo(values[..., 0 : 2 * edge_len], (("scol", 1),), 1)
    vertical = with_halo(values[..., 2 * edge_len :], (("srow", 0),), 1)
    west_side = sideways[:, :-2, :, edge_len : 2 * edge_len]
    east_side = sideways[:, 2:, :, 0:edge_len]
    south_side = vertical[:-2, :, :, edge_len : 2 * edge_len]
    north_side = vertical[2:, :, :, 0:edge_len]
    return jnp.concatenate([west_side, east_side, south_side, north_side], axis=-1)


def jump(values, partner):
    edge_len = values.shape[-1] // 4
    facing = facing_edges(values)
    offset = jnp.arange(values.shape[-1], dtype=jnp.int32) // edge_len * edge_len
    position = jnp.clip(partner, 0, edge_len - 1) + offset
    position = jnp.broadcast_to(position[:, :, None, :], values.shape)
    picked = jnp.take_along_axis(facing, position, axis=-1)
    return jnp.where(partner[:, :, None, :] >= 0, values - picked, jnp.zeros_like(values))


def apply_inverse(values, local_inverse, corner_coupling, coarse_inverse):
    sub_rows, sub_cols, rhs_count, width = values.shape
    blocks = jnp.einsum("ijab,ijrb->ijra", local_inverse, values, precision=precise)
    coarse_in = jnp.einsum("ijb,ijrb->ijr", corner_coupling, values, precision=precise)
    coarse_in = coarse_in.reshape(sub_rows * sub_cols, rhs_count)
    band_rows = coarse_inverse[0]
    coarse_out = jnp.dot(
        band_rows,
        lax.all_gather(coarse_in, "scol", axis=0, tiled=True),
        precision=precise,
        preferred_element_type=jnp.float32,
    )
    coarse_out = coarse_out.reshape(sub_rows, sub_cols, rhs_count)
    return blocks + corner_coupling[:, :, None, :] * coarse_out[..., None]


def inner(left, right):
    return jnp.sum(left * right, axis=(0, 1, 3))


def global_sums(first_dot, second_dot):
    return lax.psum((first_dot, second_dot), ("srow", "scol"))


def scaled(coef, values):
    return coef[None, None, :, None] * values


def body(loads, local_inverse, dirichlet, corner_coupling, coarse_inverse, partner):

    def operator(values):
        spread = jump(values, partner)
        return jump(apply_inverse(spread, local_inverse, corner_coupling, coarse_inverse), partner)

    def precond(values):
        spread = jump(values, partner)
        return jump(jnp.einsum("ijab,ijrb->ijra", dirichlet, spread, precision=precise), partner)

    right = operator(loads)
    multipliers = jnp.zeros_like(right)
    residual = right
    precon = precond(residual)
    image = operator(precon)
    gamma, curvature = global_sums(inner(residual, precon), inner(precon, image))
    step_size = gamma / curvature
    search = precon
    along = image
    for iteration in range(ITERS):
        multipliers = multipliers + scaled(step_size, search)
        residual = residual - scaled(step_size, along)
        if iteration + 1 < ITERS:
            precon = precond(residual)
            image = operator(precon)
            gamma_new, curvature = global_sums(inner(residual, precon), inner(precon, image))
            dir_ratio = gamma_new / gamma
            step_size = gamma_new / (curvature - dir_ratio * gamma_new / step_size)
            search = precon + scaled(dir_ratio, search)
            along = image + scaled(dir_ratio, along)
            gamma = gamma_new
    return (multipliers, residual)


def solution(mesh):
    return jax.shard_map(
        body,
        mesh=mesh,
        in_specs=(
            P("srow", "scol", None, None),
            P("srow", "scol", None, None),
            P("srow", "scol", None, None),
            P("srow", "scol", None),
            P("srow", "scol", None),
            P("srow", "scol", None),
        ),
        out_specs=(P("srow", "scol", None, None), P("srow", "scol", None, None)),
        check_vma=False,
    )
```

profile of v0, /device:TPU:0, one launch (start us, length us, event | category | flops | bytes accessed | tf_op | source)
XLA Modules:
  0.0 464.1 jit_solution(16173901481340105120)
XLA Ops:
  2.0 1.9 collective-permute-start.3
  4.0 2.3 collective-permute-start
  6.2 3.1 collective-permute-start.1
  10.9 9.6 %gather_fusion = f32[1024]{0:T(1024)S(1)} fusion(f32[2,4,128]{2,1,0:T(4,128)S(1)} %fusion.69, s32[1024]{0:T(1024)S(1)} %bitcast.196), kind=kCustom, calls=%fused_computation.clone | custom fusion | bytes 20480 | tf_op jit(solution)/shard_map/jit(take_along_axis)/gather | solution.py:43
  21.3 21.1 %all-gather = f32[8,2,4]{2,1,0:T(2,128)S(1)} all-gather(f32[1,2,4]{2,1,0:T(2,128)S(1)} %bitcast.256), channel_id=1, replica_groups=mesh['srow'=4,'scol'=8] {'scol'}, dimensions={0}, use_global_device_ids=true | all-gather | bytes 288 | tf_op jit(solution)/shard_map/all_gather | solution.py:55
  43.6 1.7 collective-permute-start.7
  45.4 4.7 %collective-permute-start.5 = (f32[1,1,4,64]{3,2,1,0:T(4,128)S(1)}, f32[1,1,4,64]{3,2,1,0:T(4,128)S(1)}, u32[]{:S(2)}, u32[]{:S(2)}) collective-permute-start(f32[1,1,4,64]{3,2,1,0:T(4,128)S(1)} %get-tuple-element.76), channel_id=1, source_target_pairs={{1,0},{2,1},{3,2},{4,3},{5,4},{6,5},{7,6},{0,7},{9,8},{10,9},{11,1... | collective-permute-start | bytes 3080 | tf_op jit(solution)/shard_map/ppermute | solution.py:19
  50.2 1.5 collective-permute-done.4
  51.7 9.6 %gather_fusion.1 = f32[1024]{0:T(1024)S(1)} fusion(f32[2,4,128]{2,1,0:T(4,128)S(1)} %fusion.65, s32[1024]{0:T(1024)S(1)} %bitcast.197), kind=kCustom, calls=%fused_computation.1.clone | custom fusion | bytes 20480 | tf_op jit(solution)/shard_map/jit(take_along_axis)/gather | solution.py:43
  61.5 1.7 collective-permute-start.11
  63.2 4.7 %collective-permute-start.9 = (f32[1,1,4,64]{3,2,1,0:T(4,128)S(1)}, f32[1,1,4,64]{3,2,1,0:T(4,128)S(1)}, u32[]{:S(2)}, u32[]{:S(2)}) collective-permute-start(f32[1,1,4,64]{3,2,1,0:T(4,128)S(1)} %get-tuple-element.72), channel_id=1, source_target_pairs={{1,0},{2,1},{3,2},{4,3},{5,4},{6,5},{7,6},{0,7},{9,8},{10,9},{11,1... | collective-permute-start | bytes 3080 | tf_op jit(solution)/shard_map/ppermute | solution.py:19
  68.0 1.5 collective-permute-done.8
  69.6 9.6 %gather_fusion.2 = f32[1024]{0:T(1024)S(1)} fusion(f32[2,4,128]{2,1,0:T(4,128)S(1)} %fusion.61, s32[1024]{0:T(1024)S(1)} %bitcast.198), kind=kCustom, calls=%fused_computation.2.clone | custom fusion | bytes 20480 | tf_op jit(solution)/shard_map/jit(take_along_axis)/gather | solution.py:43
  79.6 1.8 collective-permute-start.15
  81.3 4.7 %collective-permute-start.13 = (f32[1,1,4,64]{3,2,1,0:T(4,128)S(1)}, f32[1,1,4,64]{3,2,1,0:T(4,128)S(1)}, u32[]{:S(2)}, u32[]{:S(2)}) collective-permute-start(f32[1,1,4,64]{3,2,1,0:T(4,128)S(1)} %get-tuple-element.68), channel_id=1, source_target_pairs={{1,0},{2,1},{3,2},{4,3},{5,4},{6,5},{7,6},{0,7},{9,8},{10,9},{11,1... | collective-permute-start | bytes 3080 | tf_op jit(solution)/shard_map/ppermute | solution.py:19
  86.1 1.5 collective-permute-done.12
  87.7 9.6 %gather_fusion.3 = f32[1024]{0:T(1024)S(1)} fusion(f32[2,4,128]{2,1,0:T(4,128)S(1)} %fusion.57, s32[1024]{0:T(1024)S(1)} %bitcast.199), kind=kCustom, calls=%fused_computation.3.clone | custom fusion | bytes 20480 | tf_op jit(solution)/shard_map/jit(take_along_axis)/gather | solution.py:43
  97.4 1.7 collective-permute-start.19
  99.2 4.7 %collective-permute-start.17 = (f32[1,1,4,64]{3,2,1,0:T(4,128)S(1)}, f32[1,1,4,64]{3,2,1,0:T(4,128)S(1)}, u32[]{:S(2)}, u32[]{:S(2)}) collective-permute-start(f32[1,1,4,64]{3,2,1,0:T(4,128)S(1)} %get-tuple-element.64), channel_id=1, source_target_pairs={{1,0},{2,1},{3,2},{4,3},{5,4},{6,5},{7,6},{0,7},{9,8},{10,9},{11,1... | collective-permute-start | bytes 3080 | tf_op jit(solution)/shard_map/ppermute | solution.py:19
  104.0 1.5 collective-permute-done.16
  105.5 9.6 %gather_fusion.4 = f32[1024]{0:T(1024)S(1)} fusion(f32[2,4,128]{2,1,0:T(4,128)S(1)} %fusion.53, s32[1024]{0:T(1024)S(1)} %bitcast.200), kind=kCustom, calls=%fused_computation.4.clone | custom fusion | bytes 20480 | tf_op jit(solution)/shard_map/jit(take_along_axis)/gather | solution.py:43
  115.3 21.0 %all-gather.1 = f32[8,2,4]{2,1,0:T(2,128)S(1)} all-gather(f32[1,2,4]{2,1,0:T(2,128)S(1)} %bitcast.257), channel_id=1, replica_groups=mesh['srow'=4,'scol'=8] {'scol'}, dimensions={0}, use_global_device_ids=true | all-gather | bytes 288 | tf_op jit(solution)/shard_map/all_gather | solution.py:55
  136.8 1.7 collective-permute-start.23
  138.6 4.7 %collective-permute-start.21 = (f32[1,1,4,64]{3,2,1,0:T(4,128)S(1)}, f32[1,1,4,64]{3,2,1,0:T(4,128)S(1)}, u32[]{:S(2)}, u32[]{:S(2)}) collective-permute-start(f32[1,1,4,64]{3,2,1,0:T(4,128)S(1)} %get-tuple-element.60), channel_id=1, source_target_pairs={{1,0},{2,1},{3,2},{4,3},{5,4},{6,5},{7,6},{0,7},{9,8},{10,9},{11,1... | collective-permute-start | bytes 3080 | tf_op jit(solution)/shard_map/ppermute | solution.py:19
  143.4 1.5 collective-permute-done.20
  144.9 9.6 %gather_fusion.5 = f32[1024]{0:T(1024)S(1)} fusion(f32[2,4,128]{2,1,0:T(4,128)S(1)} %fusion.49, s32[1024]{0:T(1024)S(1)} %bitcast.201), kind=kCustom, calls=%fused_computation.5.clone | custom fusion | bytes 20480 | tf_op jit(solution)/shard_map/jit(take_along_axis)/gather | solution.py:43
  154.7 40.2 %all-reduce.2 = (f32[4]{0:T(128)S(1)}, f32[4]{0:T(128)S(1)}) all-reduce(f32[4]{0:T(128)S(1)} %get-tuple-element.8, f32[4]{0:T(128)S(1)} %get-tuple-element.7), channel_id=1, replica_groups=mesh['srow'=4,'scol'=8] {'srow','scol'}, use_global_device_ids=true, to_apply=%region_1.3 | all-reduce | flops 8 | bytes 64 | tf_op jit(solution)/shard_map/psum | solution.py:68
  195.1 1.7 collective-permute-start.27
  196.8 2.3 collective-permute-start.24
  199.1 2.4 collective-permute-start.25
  201.6 1.5 collective-permute-done.24
  203.2 9.6 %gather_fusion.6 = f32[1024]{0:T(1024)S(1)} fusion(f32[2,4,128]{2,1,0:T(4,128)S(1)} %fusion.45, s32[1024]{0:T(1024)S(1)} %bitcast.202), kind=kCustom, calls=%fused_computation.6.clone | custom fusion | bytes 20480 | tf_op jit(solution)/shard_map/jit(take_along_axis)/gather | solution.py:43
  213.2 1.8 collective-permute-start.31
  214.9 1.8 collective-permute-start.28
  216.7 2.9 collective-permute-start.29
  219.7 1.5 collective-permute-done.28
  221.3 9.6 %gather_fusion.7 = f32[1024]{0:T(1024)S(1)} fusion(f32[2,4,128]{2,1,0:T(4,128)S(1)} %fusion.41, s32[1024]{0:T(1024)S(1)} %bitcast.203), kind=kCustom, calls=%fused_computation.7.clone | custom fusion | bytes 20480 | tf_op jit(solution)/shard_map/jit(take_along_axis)/gather | solution.py:43
  231.0 1.7 collective-permute-start.35
  234.1 3.4 collective-permute-start.33
  237.6 1.5 collective-permute-done.32
  239.1 9.6 %gather_fusion.8 = f32[1024]{0:T(1024)S(1)} fusion(f32[2,4,128]{2,1,0:T(4,128)S(1)} %fusion.37, s32[1024]{0:T(1024)S(1)} %bitcast.204), kind=kCustom, calls=%fused_computation.8.clone | custom fusion | bytes 20480 | tf_op jit(solution)/shard_map/jit(take_along_axis)/gather | solution.py:43
  248.9 21.0 %all-gather.2 = f32[8,2,4]{2,1,0:T(2,128)S(1)} all-gather(f32[1,2,4]{2,1,0:T(2,128)S(1)} %bitcast.258), channel_id=1, replica_groups=mesh['srow'=4,'scol'=8] {'scol'}, dimensions={0}, use_global_device_ids=true | all-gather | bytes 288 | tf_op jit(solution)/shard_map/all_gather | solution.py:55
  270.4 1.7 collective-permute-start.39
  272.2 4.7 %collective-permute-start.37 = (f32[1,1,4,64]{3,2,1,0:T(4,128)S(1)}, f32[1,1,4,64]{3,2,1,0:T(4,128)S(1)}, u32[]{:S(2)}, u32[]{:S(2)}) collective-permute-start(f32[1,1,4,64]{3,2,1,0:T(4,128)S(1)} %get-tuple-element.44), channel_id=1, source_target_pairs={{1,0},{2,1},{3,2},{4,3},{5,4},{6,5},{7,6},{0,7},{9,8},{10,9},{11,1... | collective-permute-start | bytes 3080 | tf_op jit(solution)/shard_map/ppermute | solution.py:19
  278.5 9.6 %gather_fusion.9 = f32[1024]{0:T(1024)S(1)} fusion(f32[2,4,128]{2,1,0:T(4,128)S(1)} %fusion.33, s32[1024]{0:T(1024)S(1)} %bitcast.205), kind=kCustom, calls=%fused_computation.9.clone | custom fusion | bytes 20480 | tf_op jit(solution)/shard_map/jit(take_along_axis)/gather | solution.py:43
  288.3 40.8 %all-reduce.1 = (f32[4]{0:T(128)S(1)}, f32[4]{0:T(128)S(1)}) all-reduce(f32[4]{0:T(128)S(1)} %get-tuple-element.6, f32[4]{0:T(128)S(1)} %get-tuple-element.5), channel_id=1, replica_groups=mesh['srow'=4,'scol'=8] {'srow','scol'}, use_global_device_ids=true, to_apply=%region_5.7 | all-reduce | flops 8 | bytes 64 | tf_op jit(solution)/shard_map/psum | solution.py:68
  329.3 1.8 collective-permute-start.43
  331.1 2.3 collective-permute-start.40
  333.3 2.4 collective-permute-start.41
  337.4 9.6 %gather_fusion.10 = f32[1024]{0:T(1024)S(1)} fusion(f32[2,4,128]{2,1,0:T(4,128)S(1)} %fusion.29, s32[1024]{0:T(1024)S(1)} %bitcast.206), kind=kCustom, calls=%fused_computation.10.clone | custom fusion | bytes 20480 | tf_op jit(solution)/shard_map/jit(take_along_axis)/gather | solution.py:43
  347.4 1.8 collective-permute-start.47
  349.2 1.8 collective-permute-start.44
  351.0 2.9 collective-permute-start.45
  354.0 1.5 collective-permute-done.44
  355.5 9.6 %gather_fusion.11 = f32[1024]{0:T(1024)S(1)} fusion(f32[2,4,128]{2,1,0:T(4,128)S(1)} %fusion.25, s32[1024]{0:T(1024)S(1)} %bitcast.207), kind=kCustom, calls=%fused_computation.11.clone | custom fusion | bytes 20480 | tf_op jit(solution)/shard_map/jit(take_along_axis)/gather | solution.py:43
  365.3 1.7 collective-permute-start.51
  368.4 3.4 collective-permute-start.49
  371.8 1.5 collective-permute-done.48
  373.4 9.6 %gather_fusion.12 = f32[1024]{0:T(1024)S(1)} fusion(f32[2,4,128]{2,1,0:T(4,128)S(1)} %fusion.21, s32[1024]{0:T(1024)S(1)} %bitcast.208), kind=kCustom, calls=%fused_computation.12.clone | custom fusion | bytes 20480 | tf_op jit(solution)/shard_map/jit(take_along_axis)/gather | solution.py:43
  383.1 21.0 %all-gather.3 = f32[8,2,4]{2,1,0:T(2,128)S(1)} all-gather(f32[1,2,4]{2,1,0:T(2,128)S(1)} %bitcast.259), channel_id=1, replica_groups=mesh['srow'=4,'scol'=8] {'scol'}, dimensions={0}, use_global_device_ids=true | all-gather | bytes 288 | tf_op jit(solution)/shard_map/all_gather | solution.py:55
  404.7 1.7 collective-permute-start.55
  406.4 4.7 %collective-permute-start.53 = (f32[1,1,4,64]{3,2,1,0:T(4,128)S(1)}, f32[1,1,4,64]{3,2,1,0:T(4,128)S(1)}, u32[]{:S(2)}, u32[]{:S(2)}) collective-permute-start(f32[1,1,4,64]{3,2,1,0:T(4,128)S(1)} %get-tuple-element.28), channel_id=1, source_target_pairs={{1,0},{2,1},{3,2},{4,3},{5,4},{6,5},{7,6},{0,7},{9,8},{10,9},{11,1... | collective-permute-start | bytes 3080 | tf_op jit(solution)/shard_map/ppermute | solution.py:19
  412.8 9.6 %gather_fusion.13 = f32[1024]{0:T(1024)S(1)} fusion(f32[2,4,128]{2,1,0:T(4,128)S(1)} %fusion.17, s32[1024]{0:T(1024)S(1)} %bitcast.209), kind=kCustom, calls=%fused_computation.13.clone | custom fusion | bytes 20480 | tf_op jit(solution)/shard_map/jit(take_along_axis)/gather | solution.py:43
  422.5 40.8 %all-reduce = (f32[4]{0:T(128)S(1)}, f32[4]{0:T(128)S(1)}) all-reduce(f32[4]{0:T(128)S(1)} %get-tuple-element.4, f32[4]{0:T(128)S(1)} %get-tuple-element.3), channel_id=1, replica_groups=mesh['srow'=4,'scol'=8] {'srow','scol'}, use_global_device_ids=true, to_apply=%region_9.11 | all-reduce | flops 8 | bytes 64 | tf_op jit(solution)/shard_map/psum | solution.py:68
  (171 shorter events, 19.1 us)
Async XLA Ops:
  0.6 42.6 %copy-start = (f32[1,2,128,128]{3,2,1,0:T(8,128)S(1)}, f32[1,2,128,128]{3,2,1,0:T(8,128)}, u32[]{:S(2)}) copy-start(f32[1,2,128,128]{3,2,1,0:T(8,128)} %param.9) | copy-start | bytes 393220
  0.6 3.3 copy-start.2
  1.5 7.9 %collective-permute-start.2 = (f32[1,2,4,64]{3,2,1,0:T(4,128)S(1)}, f32[1,2,4,64]{3,2,1,0:T(4,128)S(1)}, u32[]{:S(2)}, u32[]{:S(2)}) collective-permute-start(f32[1,2,4,64]{3,2,1,0:T(4,128)S(1)} %get-tuple-element.77), channel_id=1, source_target_pairs={{0,8},{8,16},{16,24},{24,0},{1,9},{9,17},{17,25},{25,1},{2,10},{10... | collective-permute-start | bytes 6152 | tf_op jit(solution)/shard_map/ppermute | solution.py:17
  2.0 8.8 %collective-permute-start.3 = (f32[1,2,4,64]{3,2,1,0:T(4,128)S(1)}, f32[1,2,4,64]{3,2,1,0:T(4,128)S(1)}, u32[]{:S(2)}, u32[]{:S(2)}) collective-permute-start(f32[1,2,4,64]{3,2,1,0:T(4,128)S(1)} %get-tuple-element.77), channel_id=1, source_target_pairs={{8,0},{16,8},{24,16},{0,24},{9,1},{17,9},{25,17},{1,25},{10,2},{18... | collective-permute-start | bytes 6152 | tf_op jit(solution)/shard_map/ppermute | solution.py:19
  4.0 6.9 %collective-permute-start = (f32[1,1,4,64]{3,2,1,0:T(4,128)S(1)}, f32[1,1,4,64]{3,2,1,0:T(4,128)S(1)}, u32[]{:S(2)}, u32[]{:S(2)}) collective-permute-start(f32[1,1,4,64]{3,2,1,0:T(4,128)S(1)} %get-tuple-element.79), channel_id=1, source_target_pairs={{0,1},{1,2},{2,3},{3,4},{4,5},{5,6},{6,7},{7,0},{8,9},{9,10},{10,1... | collective-permute-start | bytes 3080 | tf_op jit(solution)/shard_map/ppermute | solution.py:17
  6.2 3.1 copy-start.5
  6.2 4.6 collective-permute-start.1
  20.5 0.7 copy-start.3
  42.4 0.7 copy-start.4
  43.6 6.5 %collective-permute-start.6 = (f32[1,2,4,64]{3,2,1,0:T(4,128)S(1)}, f32[1,2,4,64]{3,2,1,0:T(4,128)S(1)}, u32[]{:S(2)}, u32[]{:S(2)}) collective-permute-start(f32[1,2,4,64]{3,2,1,0:T(4,128)S(1)} %get-tuple-element.73), channel_id=1, source_target_pairs={{0,8},{8,16},{16,24},{24,0},{1,9},{9,17},{17,25},{25,1},{2,10},{10... | collective-permute-start | bytes 6152 | tf_op jit(solution)/shard_map/ppermute | solution.py:17
  43.6 8.0 %collective-permute-start.7 = (f32[1,2,4,64]{3,2,1,0:T(4,128)S(1)}, f32[1,2,4,64]{3,2,1,0:T(4,128)S(1)}, u32[]{:S(2)}, u32[]{:S(2)}) collective-permute-start(f32[1,2,4,64]{3,2,1,0:T(4,128)S(1)} %get-tuple-element.73), channel_id=1, source_target_pairs={{8,0},{16,8},{24,16},{0,24},{9,1},{17,9},{25,17},{1,25},{10,2},{18... | collective-permute-start | bytes 6152 | tf_op jit(solution)/shard_map/ppermute | solution.py:19
  45.4 6.3 %collective-permute-start.4 = (f32[1,1,4,64]{3,2,1,0:T(4,128)S(1)}, f32[1,1,4,64]{3,2,1,0:T(4,128)S(1)}, u32[]{:S(2)}, u32[]{:S(2)}) collective-permute-start(f32[1,1,4,64]{3,2,1,0:T(4,128)S(1)} %get-tuple-element.75), channel_id=1, source_target_pairs={{0,1},{1,2},{2,3},{3,4},{4,5},{5,6},{6,7},{7,0},{8,9},{9,10},{10,1... | collective-permute-start | bytes 3080 | tf_op jit(solution)/shard_map/ppermute | solution.py:17
  45.4 6.3 %collective-permute-start.5 = (f32[1,1,4,64]{3,2,1,0:T(4,128)S(1)}, f32[1,1,4,64]{3,2,1,0:T(4,128)S(1)}, u32[]{:S(2)}, u32[]{:S(2)}) collective-permute-start(f32[1,1,4,64]{3,2,1,0:T(4,128)S(1)} %get-tuple-element.76), channel_id=1, source_target_pairs={{1,0},{2,1},{3,2},{4,3},{5,4},{6,5},{7,6},{0,7},{9,8},{10,9},{11,1... | collective-permute-start | bytes 3080 | tf_op jit(solution)/shard_map/ppermute | solution.py:19
  61.4 6.5 %collective-permute-start.10 = (f32[1,2,4,64]{3,2,1,0:T(4,128)S(1)}, f32[1,2,4,64]{3,2,1,0:T(4,128)S(1)}, u32[]{:S(2)}, u32[]{:S(2)}) collective-permute-start(f32[1,2,4,64]{3,2,1,0:T(4,128)S(1)} %get-tuple-element.69), channel_id=1, source_target_pairs={{0,8},{8,16},{16,24},{24,0},{1,9},{9,17},{17,25},{25,1},{2,10},{10... | collective-permute-start | bytes 6152 | tf_op jit(solution)/shard_map/ppermute | solution.py:17
  61.5 8.0 %collective-permute-start.11 = (f32[1,2,4,64]{3,2,1,0:T(4,128)S(1)}, f32[1,2,4,64]{3,2,1,0:T(4,128)S(1)}, u32[]{:S(2)}, u32[]{:S(2)}) collective-permute-start(f32[1,2,4,64]{3,2,1,0:T(4,128)S(1)} %get-tuple-element.69), channel_id=1, source_target_pairs={{8,0},{16,8},{24,16},{0,24},{9,1},{17,9},{25,17},{1,25},{10,2},{18... | collective-permute-start | bytes 6152 | tf_op jit(solution)/shard_map/ppermute | solution.py:19
  63.2 6.3 %collective-permute-start.8 = (f32[1,1,4,64]{3,2,1,0:T(4,128)S(1)}, f32[1,1,4,64]{3,2,1,0:T(4,128)S(1)}, u32[]{:S(2)}, u32[]{:S(2)}) collective-permute-start(f32[1,1,4,64]{3,2,1,0:T(4,128)S(1)} %get-tuple-element.71), channel_id=1, source_target_pairs={{0,1},{1,2},{2,3},{3,4},{4,5},{5,6},{6,7},{7,0},{8,9},{9,10},{10,1... | collective-permute-start | bytes 3080 | tf_op jit(solution)/shard_map/ppermute | solution.py:17
  63.2 6.3 %collective-permute-start.9 = (f32[1,1,4,64]{3,2,1,0:T(4,128)S(1)}, f32[1,1,4,64]{3,2,1,0:T(4,128)S(1)}, u32[]{:S(2)}, u32[]{:S(2)}) collective-permute-start(f32[1,1,4,64]{3,2,1,0:T(4,128)S(1)} %get-tuple-element.72), channel_id=1, source_target_pairs={{1,0},{2,1},{3,2},{4,3},{5,4},{6,5},{7,6},{0,7},{9,8},{10,9},{11,1... | collective-permute-start | bytes 3080 | tf_op jit(solution)/shard_map/ppermute | solution.py:19
  69.6 9.6 %copy-start.1 = (f32[1,2,128,128]{3,2,1,0:T(8,128)S(1)}, f32[1,2,128,128]{3,2,1,0:T(8,128)}, u32[]{:S(2)}) copy-start(f32[1,2,128,128]{3,2,1,0:T(8,128)} %param.10) | copy-start | bytes 393220
  79.6 6.5 %collective-permute-start.14 = (f32[1,2,4,64]{3,2,1,0:T(4,128)S(1)}, f32[1,2,4,64]{3,2,1,0:T(4,128)S(1)}, u32[]{:S(2)}, u32[]{:S(2)}) collective-permute-start(f32[1,2,4,64]{3,2,1,0:T(4,128)S(1)} %get-tuple-element.65), channel_id=1, source_target_pairs={{0,8},{8,16},{16,24},{24,0},{1,9},{9,17},{17,25},{25,1},{2,10},{10... | collective-permute-start | bytes 6152 | tf_op jit(solution)/shard_map/ppermute | solution.py:17
  79.6 8.0 %collective-permute-start.15 = (f32[1,2,4,64]{3,2,1,0:T(4,128)S(1)}, f32[1,2,4,64]{3,2,1,0:T(4,128)S(1)}, u32[]{:S(2)}, u32[]{:S(2)}) collective-permute-start(f32[1,2,4,64]{3,2,1,0:T(4,128)S(1)} %get-tuple-element.65), channel_id=1, source_target_pairs={{8,0},{16,8},{24,16},{0,24},{9,1},{17,9},{25,17},{1,25},{10,2},{18... | collective-permute-start | bytes 6152 | tf_op jit(solution)/shard_map/ppermute | solution.py:19
  81.3 6.3 %collective-permute-start.12 = (f32[1,1,4,64]{3,2,1,0:T(4,128)S(1)}, f32[1,1,4,64]{3,2,1,0:T(4,128)S(1)}, u32[]{:S(2)}, u32[]{:S(2)}) collective-permute-start(f32[1,1,4,64]{3,2,1,0:T(4,128)S(1)} %get-tuple-element.67), channel_id=1, source_target_pairs={{0,1},{1,2},{2,3},{3,4},{4,5},{5,6},{6,7},{7,0},{8,9},{9,10},{10,1... | collective-permute-start | bytes 3080 | tf_op jit(solution)/shard_map/ppermute | solution.py:17
  81.3 6.3 %collective-permute-start.13 = (f32[1,1,4,64]{3,2,1,0:T(4,128)S(1)}, f32[1,1,4,64]{3,2,1,0:T(4,128)S(1)}, u32[]{:S(2)}, u32[]{:S(2)}) collective-permute-start(f32[1,1,4,64]{3,2,1,0:T(4,128)S(1)} %get-tuple-element.68), channel_id=1, source_target_pairs={{1,0},{2,1},{3,2},{4,3},{5,4},{6,5},{7,6},{0,7},{9,8},{10,9},{11,1... | collective-permute-start | bytes 3080 | tf_op jit(solution)/shard_map/ppermute | solution.py:19
  97.4 6.5 %collective-permute-start.18 = (f32[1,2,4,64]{3,2,1,0:T(4,128)S(1)}, f32[1,2,4,64]{3,2,1,0:T(4,128)S(1)}, u32[]{:S(2)}, u32[]{:S(2)}) collective-permute-start(f32[1,2,4,64]{3,2,1,0:T(4,128)S(1)} %get-tuple-element.61), channel_id=1, source_target_pairs={{0,8},{8,16},{16,24},{24,0},{1,9},{9,17},{17,25},{25,1},{2,10},{10... | collective-permute-start | bytes 6152 | tf_op jit(solution)/shard_map/ppermute | solution.py:17
  97.4 8.0 %collective-permute-start.19 = (f32[1,2,4,64]{3,2,1,0:T(4,128)S(1)}, f32[1,2,4,64]{3,2,1,0:T(4,128)S(1)}, u32[]{:S(2)}, u32[]{:S(2)}) collective-permute-start(f32[1,2,4,64]{3,2,1,0:T(4,128)S(1)} %get-tuple-element.61), channel_id=1, source_target_pairs={{8,0},{16,8},{24,16},{0,24},{9,1},{17,9},{25,17},{1,25},{10,2},{18... | collective-permute-start | bytes 6152 | tf_op jit(solution)/shard_map/ppermute | solution.py:19
  99.2 6.3 %collective-permute-start.16 = (f32[1,1,4,64]{3,2,1,0:T(4,128)S(1)}, f32[1,1,4,64]{3,2,1,0:T(4,128)S(1)}, u32[]{:S(2)}, u32[]{:S(2)}) collective-permute-start(f32[1,1,4,64]{3,2,1,0:T(4,128)S(1)} %get-tuple-element.63), channel_id=1, source_target_pairs={{0,1},{1,2},{2,3},{3,4},{4,5},{5,6},{6,7},{7,0},{8,9},{9,10},{10,1... | collective-permute-start | bytes 3080 | tf_op jit(solution)/shard_map/ppermute | solution.py:17
  99.2 6.3 %collective-permute-start.17 = (f32[1,1,4,64]{3,2,1,0:T(4,128)S(1)}, f32[1,1,4,64]{3,2,1,0:T(4,128)S(1)}, u32[]{:S(2)}, u32[]{:S(2)}) collective-permute-start(f32[1,1,4,64]{3,2,1,0:T(4,128)S(1)} %get-tuple-element.64), channel_id=1, source_target_pairs={{1,0},{2,1},{3,2},{4,3},{5,4},{6,5},{7,6},{0,7},{9,8},{10,9},{11,1... | collective-permute-start | bytes 3080 | tf_op jit(solution)/shard_map/ppermute | solution.py:19
  136.8 6.5 %collective-permute-start.22 = (f32[1,2,4,64]{3,2,1,0:T(4,128)S(1)}, f32[1,2,4,64]{3,2,1,0:T(4,128)S(1)}, u32[]{:S(2)}, u32[]{:S(2)}) collective-permute-start(f32[1,2,4,64]{3,2,1,0:T(4,128)S(1)} %get-tuple-element.57), channel_id=1, source_target_pairs={{0,8},{8,16},{16,24},{24,0},{1,9},{9,17},{17,25},{25,1},{2,10},{10... | collective-permute-start | bytes 6152 | tf_op jit(solution)/shard_map/ppermute | solution.py:17
  136.8 8.0 %collective-permute-start.23 = (f32[1,2,4,64]{3,2,1,0:T(4,128)S(1)}, f32[1,2,4,64]{3,2,1,0:T(4,128)S(1)}, u32[]{:S(2)}, u32[]{:S(2)}) collective-permute-start(f32[1,2,4,64]{3,2,1,0:T(4,128)S(1)} %get-tuple-element.57), channel_id=1, source_target_pairs={{8,0},{16,8},{24,16},{0,24},{9,1},{17,9},{25,17},{1,25},{10,2},{18... | collective-permute-start | bytes 6152 | tf_op jit(solution)/shard_map/ppermute | solution.py:19
  138.6 6.3 %collective-permute-start.20 = (f32[1,1,4,64]{3,2,1,0:T(4,128)S(1)}, f32[1,1,4,64]{3,2,1,0:T(4,128)S(1)}, u32[]{:S(2)}, u32[]{:S(2)}) collective-permute-start(f32[1,1,4,64]{3,2,1,0:T(4,128)S(1)} %get-tuple-element.59), channel_id=1, source_target_pairs={{0,1},{1,2},{2,3},{3,4},{4,5},{5,6},{6,7},{7,0},{8,9},{9,10},{10,1... | collective-permute-start | bytes 3080 | tf_op jit(solution)/shard_map/ppermute | solution.py:17
  138.6 6.3 %collective-permute-start.21 = (f32[1,1,4,64]{3,2,1,0:T(4,128)S(1)}, f32[1,1,4,64]{3,2,1,0:T(4,128)S(1)}, u32[]{:S(2)}, u32[]{:S(2)}) collective-permute-start(f32[1,1,4,64]{3,2,1,0:T(4,128)S(1)} %get-tuple-element.60), channel_id=1, source_target_pairs={{1,0},{2,1},{3,2},{4,3},{5,4},{6,5},{7,6},{0,7},{9,8},{10,9},{11,1... | collective-permute-start | bytes 3080 | tf_op jit(solution)/shard_map/ppermute | solution.py:19
  195.1 6.5 %collective-permute-start.26 = (f32[1,2,4,64]{3,2,1,0:T(4,128)S(1)}, f32[1,2,4,64]{3,2,1,0:T(4,128)S(1)}, u32[]{:S(2)}, u32[]{:S(2)}) collective-permute-start(f32[1,2,4,64]{3,2,1,0:T(4,128)S(1)} %get-tuple-element.53), channel_id=1, source_target_pairs={{0,8},{8,16},{16,24},{24,0},{1,9},{9,17},{17,25},{25,1},{2,10},{10... | collective-permute-start | bytes 6152 | tf_op jit(solution)/shard_map/ppermute | solution.py:17
  195.1 8.0 %collective-permute-start.27 = (f32[1,2,4,64]{3,2,1,0:T(4,128)S(1)}, f32[1,2,4,64]{3,2,1,0:T(4,128)S(1)}, u32[]{:S(2)}, u32[]{:S(2)}) collective-permute-start(f32[1,2,4,64]{3,2,1,0:T(4,128)S(1)} %get-tuple-element.53), channel_id=1, source_target_pairs={{8,0},{16,8},{24,16},{0,24},{9,1},{17,9},{25,17},{1,25},{10,2},{18... | collective-permute-start | bytes 6152 | tf_op jit(solution)/shard_map/ppermute | solution.py:19
  196.8 6.3 %collective-permute-start.24 = (f32[1,1,4,64]{3,2,1,0:T(4,128)S(1)}, f32[1,1,4,64]{3,2,1,0:T(4,128)S(1)}, u32[]{:S(2)}, u32[]{:S(2)}) collective-permute-start(f32[1,1,4,64]{3,2,1,0:T(4,128)S(1)} %get-tuple-element.55), channel_id=1, source_target_pairs={{0,1},{1,2},{2,3},{3,4},{4,5},{5,6},{6,7},{7,0},{8,9},{9,10},{10,1... | collective-permute-start | bytes 3080 | tf_op jit(solution)/shard_map/ppermute | solution.py:17
  199.1 4.0 collective-permute-start.25
  213.2 6.5 %collective-permute-start.30 = (f32[1,2,4,64]{3,2,1,0:T(4,128)S(1)}, f32[1,2,4,64]{3,2,1,0:T(4,128)S(1)}, u32[]{:S(2)}, u32[]{:S(2)}) collective-permute-start(f32[1,2,4,64]{3,2,1,0:T(4,128)S(1)} %get-tuple-element.49), channel_id=1, source_target_pairs={{0,8},{8,16},{16,24},{24,0},{1,9},{9,17},{17,25},{25,1},{2,10},{10... | collective-permute-start | bytes 6152 | tf_op jit(solution)/shard_map/ppermute | solution.py:17
  213.2 8.0 %collective-permute-start.31 = (f32[1,2,4,64]{3,2,1,0:T(4,128)S(1)}, f32[1,2,4,64]{3,2,1,0:T(4,128)S(1)}, u32[]{:S(2)}, u32[]{:S(2)}) collective-permute-start(f32[1,2,4,64]{3,2,1,0:T(4,128)S(1)} %get-tuple-element.49), channel_id=1, source_target_pairs={{8,0},{16,8},{24,16},{0,24},{9,1},{17,9},{25,17},{1,25},{10,2},{18... | collective-permute-start | bytes 6152 | tf_op jit(solution)/shard_map/ppermute | solution.py:19
  214.9 6.3 %collective-permute-start.28 = (f32[1,1,4,64]{3,2,1,0:T(4,128)S(1)}, f32[1,1,4,64]{3,2,1,0:T(4,128)S(1)}, u32[]{:S(2)}, u32[]{:S(2)}) collective-permute-start(f32[1,1,4,64]{3,2,1,0:T(4,128)S(1)} %get-tuple-element.51), channel_id=1, source_target_pairs={{0,1},{1,2},{2,3},{3,4},{4,5},{5,6},{6,7},{7,0},{8,9},{9,10},{10,1... | collective-permute-start | bytes 3080 | tf_op jit(solution)/shard_map/ppermute | solution.py:17
  216.7 4.5 collective-permute-start.29
  231.0 6.5 %collective-permute-start.34 = (f32[1,2,4,64]{3,2,1,0:T(4,128)S(1)}, f32[1,2,4,64]{3,2,1,0:T(4,128)S(1)}, u32[]{:S(2)}, u32[]{:S(2)}) collective-permute-start(f32[1,2,4,64]{3,2,1,0:T(4,128)S(1)} %get-tuple-element.45), channel_id=1, source_target_pairs={{0,8},{8,16},{16,24},{24,0},{1,9},{9,17},{17,25},{25,1},{2,10},{10... | collective-permute-start | bytes 6152 | tf_op jit(solution)/shard_map/ppermute | solution.py:17
  231.0 8.0 %collective-permute-start.35 = (f32[1,2,4,64]{3,2,1,0:T(4,128)S(1)}, f32[1,2,4,64]{3,2,1,0:T(4,128)S(1)}, u32[]{:S(2)}, u32[]{:S(2)}) collective-permute-start(f32[1,2,4,64]{3,2,1,0:T(4,128)S(1)} %get-tuple-element.45), channel_id=1, source_target_pairs={{8,0},{16,8},{24,16},{0,24},{9,1},{17,9},{25,17},{1,25},{10,2},{18... | collective-permute-start | bytes 6152 | tf_op jit(solution)/shard_map/ppermute | solution.py:19
  232.8 6.3 %collective-permute-start.32 = (f32[1,1,4,64]{3,2,1,0:T(4,128)S(1)}, f32[1,1,4,64]{3,2,1,0:T(4,128)S(1)}, u32[]{:S(2)}, u32[]{:S(2)}) collective-permute-start(f32[1,1,4,64]{3,2,1,0:T(4,128)S(1)} %get-tuple-element.47), channel_id=1, source_target_pairs={{0,1},{1,2},{2,3},{3,4},{4,5},{5,6},{6,7},{7,0},{8,9},{9,10},{10,1... | collective-permute-start | bytes 3080 | tf_op jit(solution)/shard_map/ppermute | solution.py:17
  234.1 4.9 %collective-permute-start.33 = (f32[1,1,4,64]{3,2,1,0:T(4,128)S(1)}, f32[1,1,4,64]{3,2,1,0:T(4,128)S(1)}, u32[]{:S(2)}, u32[]{:S(2)}) collective-permute-start(f32[1,1,4,64]{3,2,1,0:T(4,128)S(1)} %get-tuple-element.48), channel_id=1, source_target_pairs={{1,0},{2,1},{3,2},{4,3},{5,4},{6,5},{7,6},{0,7},{9,8},{10,9},{11,1... | collective-permute-start | bytes 3080 | tf_op jit(solution)/shard_map/ppermute | solution.py:19
  270.4 6.5 %collective-permute-start.38 = (f32[1,2,4,64]{3,2,1,0:T(4,128)S(1)}, f32[1,2,4,64]{3,2,1,0:T(4,128)S(1)}, u32[]{:S(2)}, u32[]{:S(2)}) collective-permute-start(f32[1,2,4,64]{3,2,1,0:T(4,128)S(1)} %get-tuple-element.41), channel_id=1, source_target_pairs={{0,8},{8,16},{16,24},{24,0},{1,9},{9,17},{17,25},{25,1},{2,10},{10... | collective-permute-start | bytes 6152 | tf_op jit(solution)/shard_map/ppermute | solution.py:17
  270.4 8.0 %collective-permute-start.39 = (f32[1,2,4,64]{3,2,1,0:T(4,128)S(1)}, f32[1,2,4,64]{3,2,1,0:T(4,128)S(1)}, u32[]{:S(2)}, u32[]{:S(2)}) collective-permute-start(f32[1,2,4,64]{3,2,1,0:T(4,128)S(1)} %get-tuple-element.41), channel_id=1, source_target_pairs={{8,0},{16,8},{24,16},{0,24},{9,1},{17,9},{25,17},{1,25},{10,2},{18... | collective-permute-start | bytes 6152 | tf_op jit(solution)/shard_map/ppermute | solution.py:19
  272.2 6.3 %collective-permute-start.36 = (f32[1,1,4,64]{3,2,1,0:T(4,128)S(1)}, f32[1,1,4,64]{3,2,1,0:T(4,128)S(1)}, u32[]{:S(2)}, u32[]{:S(2)}) collective-permute-start(f32[1,1,4,64]{3,2,1,0:T(4,128)S(1)} %get-tuple-element.43), channel_id=1, source_target_pairs={{0,1},{1,2},{2,3},{3,4},{4,5},{5,6},{6,7},{7,0},{8,9},{9,10},{10,1... | collective-permute-start | bytes 3080 | tf_op jit(solution)/shard_map/ppermute | solution.py:17
  272.2 6.3 %collective-permute-start.37 = (f32[1,1,4,64]{3,2,1,0:T(4,128)S(1)}, f32[1,1,4,64]{3,2,1,0:T(4,128)S(1)}, u32[]{:S(2)}, u32[]{:S(2)}) collective-permute-start(f32[1,1,4,64]{3,2,1,0:T(4,128)S(1)} %get-tuple-element.44), channel_id=1, source_target_pairs={{1,0},{2,1},{3,2},{4,3},{5,4},{6,5},{7,6},{0,7},{9,8},{10,9},{11,1... | collective-permute-start | bytes 3080 | tf_op jit(solution)/shard_map/ppermute | solution.py:19
  329.3 6.5 %collective-permute-start.42 = (f32[1,2,4,64]{3,2,1,0:T(4,128)S(1)}, f32[1,2,4,64]{3,2,1,0:T(4,128)S(1)}, u32[]{:S(2)}, u32[]{:S(2)}) collective-permute-start(f32[1,2,4,64]{3,2,1,0:T(4,128)S(1)} %get-tuple-element.37), channel_id=1, source_target_pairs={{0,8},{8,16},{16,24},{24,0},{1,9},{9,17},{17,25},{25,1},{2,10},{10... | collective-permute-start | bytes 6152 | tf_op jit(solution)/shard_map/ppermute | solution.py:17
  329.3 8.0 %collective-permute-start.43 = (f32[1,2,4,64]{3,2,1,0:T(4,128)S(1)}, f32[1,2,4,64]{3,2,1,0:T(4,128)S(1)}, u32[]{:S(2)}, u32[]{:S(2)}) collective-permute-start(f32[1,2,4,64]{3,2,1,0:T(4,128)S(1)} %get-tuple-element.37), channel_id=1, source_target_pairs={{8,0},{16,8},{24,16},{0,24},{9,1},{17,9},{25,17},{1,25},{10,2},{18... | collective-permute-start | bytes 6152 | tf_op jit(solution)/shard_map/ppermute | solution.py:19
  331.1 6.3 %collective-permute-start.40 = (f32[1,1,4,64]{3,2,1,0:T(4,128)S(1)}, f32[1,1,4,64]{3,2,1,0:T(4,128)S(1)}, u32[]{:S(2)}, u32[]{:S(2)}) collective-permute-start(f32[1,1,4,64]{3,2,1,0:T(4,128)S(1)} %get-tuple-element.39), channel_id=1, source_target_pairs={{0,1},{1,2},{2,3},{3,4},{4,5},{5,6},{6,7},{7,0},{8,9},{9,10},{10,1... | collective-permute-start | bytes 3080 | tf_op jit(solution)/shard_map/ppermute | solution.py:17
  333.3 4.0 collective-permute-start.41
  347.4 6.5 %collective-permute-start.46 = (f32[1,2,4,64]{3,2,1,0:T(4,128)S(1)}, f32[1,2,4,64]{3,2,1,0:T(4,128)S(1)}, u32[]{:S(2)}, u32[]{:S(2)}) collective-permute-start(f32[1,2,4,64]{3,2,1,0:T(4,128)S(1)} %get-tuple-element.33), channel_id=1, source_target_pairs={{0,8},{8,16},{16,24},{24,0},{1,9},{9,17},{17,25},{25,1},{2,10},{10... | collective-permute-start | bytes 6152 | tf_op jit(solution)/shard_map/ppermute | solution.py:17
  347.4 8.0 %collective-permute-start.47 = (f32[1,2,4,64]{3,2,1,0:T(4,128)S(1)}, f32[1,2,4,64]{3,2,1,0:T(4,128)S(1)}, u32[]{:S(2)}, u32[]{:S(2)}) collective-permute-start(f32[1,2,4,64]{3,2,1,0:T(4,128)S(1)} %get-tuple-element.33), channel_id=1, source_target_pairs={{8,0},{16,8},{24,16},{0,24},{9,1},{17,9},{25,17},{1,25},{10,2},{18... | collective-permute-start | bytes 6152 | tf_op jit(solution)/shard_map/ppermute | solution.py:19
  349.2 6.3 %collective-permute-start.44 = (f32[1,1,4,64]{3,2,1,0:T(4,128)S(1)}, f32[1,1,4,64]{3,2,1,0:T(4,128)S(1)}, u32[]{:S(2)}, u32[]{:S(2)}) collective-permute-start(f32[1,1,4,64]{3,2,1,0:T(4,128)S(1)} %get-tuple-element.35), channel_id=1, source_target_pairs={{0,1},{1,2},{2,3},{3,4},{4,5},{5,6},{6,7},{7,0},{8,9},{9,10},{10,1... | collective-permute-start | bytes 3080 | tf_op jit(solution)/shard_map/ppermute | solution.py:17
  351.0 4.5 collective-permute-start.45
  365.2 6.5 %collective-permute-start.50 = (f32[1,2,4,64]{3,2,1,0:T(4,128)S(1)}, f32[1,2,4,64]{3,2,1,0:T(4,128)S(1)}, u32[]{:S(2)}, u32[]{:S(2)}) collective-permute-start(f32[1,2,4,64]{3,2,1,0:T(4,128)S(1)} %get-tuple-element.29), channel_id=1, source_target_pairs={{0,8},{8,16},{16,24},{24,0},{1,9},{9,17},{17,25},{25,1},{2,10},{10... | collective-permute-start | bytes 6152 | tf_op jit(solution)/shard_map/ppermute | solution.py:17
  365.3 8.0 %collective-permute-start.51 = (f32[1,2,4,64]{3,2,1,0:T(4,128)S(1)}, f32[1,2,4,64]{3,2,1,0:T(4,128)S(1)}, u32[]{:S(2)}, u32[]{:S(2)}) collective-permute-start(f32[1,2,4,64]{3,2,1,0:T(4,128)S(1)} %get-tuple-element.29), channel_id=1, source_target_pairs={{8,0},{16,8},{24,16},{0,24},{9,1},{17,9},{25,17},{1,25},{10,2},{18... | collective-permute-start | bytes 6152 | tf_op jit(solution)/shard_map/ppermute | solution.py:19
  367.0 6.3 %collective-permute-start.48 = (f32[1,1,4,64]{3,2,1,0:T(4,128)S(1)}, f32[1,1,4,64]{3,2,1,0:T(4,128)S(1)}, u32[]{:S(2)}, u32[]{:S(2)}) collective-permute-start(f32[1,1,4,64]{3,2,1,0:T(4,128)S(1)} %get-tuple-element.31), channel_id=1, source_target_pairs={{0,1},{1,2},{2,3},{3,4},{4,5},{5,6},{6,7},{7,0},{8,9},{9,10},{10,1... | collective-permute-start | bytes 3080 | tf_op jit(solution)/shard_map/ppermute | solution.py:17
  368.4 4.9 %collective-permute-start.49 = (f32[1,1,4,64]{3,2,1,0:T(4,128)S(1)}, f32[1,1,4,64]{3,2,1,0:T(4,128)S(1)}, u32[]{:S(2)}, u32[]{:S(2)}) collective-permute-start(f32[1,1,4,64]{3,2,1,0:T(4,128)S(1)} %get-tuple-element.32), channel_id=1, source_target_pairs={{1,0},{2,1},{3,2},{4,3},{5,4},{6,5},{7,6},{0,7},{9,8},{10,9},{11,1... | collective-permute-start | bytes 3080 | tf_op jit(solution)/shard_map/ppermute | solution.py:19
  404.6 6.5 %collective-permute-start.54 = (f32[1,2,4,64]{3,2,1,0:T(4,128)S(1)}, f32[1,2,4,64]{3,2,1,0:T(4,128)S(1)}, u32[]{:S(2)}, u32[]{:S(2)}) collective-permute-start(f32[1,2,4,64]{3,2,1,0:T(4,128)S(1)} %get-tuple-element.25), channel_id=1, source_target_pairs={{0,8},{8,16},{16,24},{24,0},{1,9},{9,17},{17,25},{25,1},{2,10},{10... | collective-permute-start | bytes 6152 | tf_op jit(solution)/shard_map/ppermute | solution.py:17
  404.7 8.0 %collective-permute-start.55 = (f32[1,2,4,64]{3,2,1,0:T(4,128)S(1)}, f32[1,2,4,64]{3,2,1,0:T(4,128)S(1)}, u32[]{:S(2)}, u32[]{:S(2)}) collective-permute-start(f32[1,2,4,64]{3,2,1,0:T(4,128)S(1)} %get-tuple-element.25), channel_id=1, source_target_pairs={{8,0},{16,8},{24,16},{0,24},{9,1},{17,9},{25,17},{1,25},{10,2},{18... | collective-permute-start | bytes 6152 | tf_op jit(solution)/shard_map/ppermute | solution.py:19
  406.4 6.3 %collective-permute-start.52 = (f32[1,1,4,64]{3,2,1,0:T(4,128)S(1)}, f32[1,1,4,64]{3,2,1,0:T(4,128)S(1)}, u32[]{:S(2)}, u32[]{:S(2)}) collective-permute-start(f32[1,1,4,64]{3,2,1,0:T(4,128)S(1)} %get-tuple-element.27), channel_id=1, source_target_pairs={{0,1},{1,2},{2,3},{3,4},{4,5},{5,6},{6,7},{7,0},{8,9},{9,10},{10,1... | collective-permute-start | bytes 3080 | tf_op jit(solution)/shard_map/ppermute | solution.py:17
  406.4 6.3 %collective-permute-start.53 = (f32[1,1,4,64]{3,2,1,0:T(4,128)S(1)}, f32[1,1,4,64]{3,2,1,0:T(4,128)S(1)}, u32[]{:S(2)}, u32[]{:S(2)}) collective-permute-start(f32[1,1,4,64]{3,2,1,0:T(4,128)S(1)} %get-tuple-element.28), channel_id=1, source_target_pairs={{1,0},{2,1},{3,2},{4,3},{5,4},{6,5},{7,6},{0,7},{9,8},{10,9},{11,1... | collective-permute-start | bytes 3080 | tf_op jit(solution)/shard_map/ppermute | solution.py:19
where the time goes:
time: 465 us; the launch traced here: 464 us
  blocking collectives  206 us (44%)
  local copies, waits for them, and re-layouts  139 us (30%)
  starting transfers between devices  92 us (20%)
  waiting for transfers between devices  20.7 us (4%)
    gather x14, local copies, waits for them, and re-layouts, jump(): picked = jnp.take_along_axis(facing, position, axis=-1)  134 us
    psum x3, blocking collectives, global_sums(): return lax.psum((first_dot, second_dot), ('srow', 'scol'))  122 us
    all_gather x4, blocking collectives, apply_inverse(): lax.all_gather(coarse_in, 'scol', axis=0, tiled=True)  84.1 us
    ppermute x28, starting transfers between devices, with_halo(): lax.ppermute(head, axis, [((i + 1) % count, i) for i in range(count)])  78.3 us
    ppermute x28, waiting for transfers between devices, with_halo(): lax.ppermute(tail, axis, [(i, (i + 1) % count) for i in range(count)])  20.7 us
    ppermute x28, starting transfers between devices, with_halo(): lax.ppermute(tail, axis, [(i, (i + 1) % count) for i in range(count)])  13.7 us
  transfers between devices with their start and end apart: 56, of which 14 were waited for; matrix products, arithmetic and copies ran while one was open for 0% of the time, Pallas kernels for 0%

commit v1 on v0

--- a/solution.py
+++ b/solution.py
@@ -65,7 +65,7 @@
 
 
 def global_sums(first_dot, second_dot):
-    return lax.psum((first_dot, second_dot), ("srow", "scol"))
+    return lax.psum(lax.psum((first_dot, second_dot), "scol"), "srow")
 
 
 def scaled(coef, values):

time: 465 us -> 425 us (0.914)
  blocking collectives: 206 us -> 167 us
    psum x3 -> x6, blocking collectives: 122 us -> 82.5 us  [global_sums(): return lax.psum(lax.psum((first_dot, second_dot), 'scol'), 'srow')]
    ppermute x28, starting transfers between devices: 13.7 us -> 2.88 us  [with_halo(): lax.ppermute(tail, axis, [(i, (i + 1) % count) for i in range(count)])]
    ppermute x28, starting transfers between devices: 78.3 us -> 89.1 us  [with_halo(): lax.ppermute(head, axis, [((i + 1) % count, i) for i in range(count)])]
where the time goes in v1:
time: 425 us
  blocking collectives  167 us (39%)
  local copies, waits for them, and re-layouts  139 us (33%)
  starting transfers between devices  92 us (22%)
  waiting for transfers between devices  20.7 us (5%)
    gather x14, local copies, waits for them, and re-layouts, jump(): picked = jnp.take_along_axis(facing, position, axis=-1)  134 us
    ppermute x28, starting transfers between devices, with_halo(): lax.ppermute(head, axis, [((i + 1) % count, i) for i in range(count)])  89.1 us
    all_gather x4, blocking collectives, apply_inverse(): lax.all_gather(coarse_in, 'scol', axis=0, tiled=True)  84.1 us
    psum x6, blocking collectives, global_sums(): return lax.psum(lax.psum((first_dot, second_dot), 'scol'), 'srow')  82.5 us
    ppermute x28, waiting for transfers between devices, with_halo(): lax.ppermute(tail, axis, [(i, (i + 1) % count) for i in range(count)])  20.7 us
  transfers between devices with their start and end apart: 56, of which 14 were waited for; matrix products, arithmetic and copies ran while one was open for 0% of the time, Pallas kernels for 0%

profile of v1, /device:TPU:0, one launch (start us, length us, event | category | flops | bytes accessed | tf_op | source)
XLA Modules:
  0.0 424.6 jit_solution(13561833450493190565)
XLA Ops:
  2.0 1.9 collective-permute-start.3
  4.0 2.3 collective-permute-start
  6.2 3.1 collective-permute-start.1
  10.9 9.6 %gather_fusion = f32[1024]{0:T(1024)S(1)} fusion(f32[2,4,128]{2,1,0:T(4,128)S(1)} %fusion.69, s32[1024]{0:T(1024)S(1)} %bitcast.196), kind=kCustom, calls=%fused_computation.clone | custom fusion | bytes 20480 | tf_op jit(solution)/shard_map/jit(take_along_axis)/gather | solution.py:43
  21.3 21.1 %all-gather = f32[8,2,4]{2,1,0:T(2,128)S(1)} all-gather(f32[1,2,4]{2,1,0:T(2,128)S(1)} %bitcast.256), channel_id=1, replica_groups=mesh['srow'=4,'scol'=8] {'scol'}, dimensions={0}, use_global_device_ids=true | all-gather | bytes 288 | tf_op jit(solution)/shard_map/all_gather | solution.py:55
  43.6 1.7 collective-permute-start.7
  45.4 4.7 %collective-permute-start.5 = (f32[1,1,4,64]{3,2,1,0:T(4,128)S(1)}, f32[1,1,4,64]{3,2,1,0:T(4,128)S(1)}, u32[]{:S(2)}, u32[]{:S(2)}) collective-permute-start(f32[1,1,4,64]{3,2,1,0:T(4,128)S(1)} %get-tuple-element.82), channel_id=1, source_target_pairs={{1,0},{2,1},{3,2},{4,3},{5,4},{6,5},{7,6},{0,7},{9,8},{10,9},{11,1... | collective-permute-start | bytes 3080 | tf_op jit(solution)/shard_map/ppermute | solution.py:19
  50.2 1.5 collective-permute-done.4
  51.7 9.6 %gather_fusion.1 = f32[1024]{0:T(1024)S(1)} fusion(f32[2,4,128]{2,1,0:T(4,128)S(1)} %fusion.65, s32[1024]{0:T(1024)S(1)} %bitcast.197), kind=kCustom, calls=%fused_computation.1.clone | custom fusion | bytes 20480 | tf_op jit(solution)/shard_map/jit(take_along_axis)/gather | solution.py:43
  61.5 1.7 collective-permute-start.11
  63.2 4.7 %collective-permute-start.9 = (f32[1,1,4,64]{3,2,1,0:T(4,128)S(1)}, f32[1,1,4,64]{3,2,1,0:T(4,128)S(1)}, u32[]{:S(2)}, u32[]{:S(2)}) collective-permute-start(f32[1,1,4,64]{3,2,1,0:T(4,128)S(1)} %get-tuple-element.78), channel_id=1, source_target_pairs={{1,0},{2,1},{3,2},{4,3},{5,4},{6,5},{7,6},{0,7},{9,8},{10,9},{11,1... | collective-permute-start | bytes 3080 | tf_op jit(solution)/shard_map/ppermute | solution.py:19
  68.0 1.5 collective-permute-done.8
  69.6 9.6 %gather_fusion.2 = f32[1024]{0:T(1024)S(1)} fusion(f32[2,4,128]{2,1,0:T(4,128)S(1)} %fusion.61, s32[1024]{0:T(1024)S(1)} %bitcast.198), kind=kCustom, calls=%fused_computation.2.clone | custom fusion | bytes 20480 | tf_op jit(solution)/shard_map/jit(take_along_axis)/gather | solution.py:43
  79.6 1.8 collective-permute-start.15
  81.3 4.7 %collective-permute-start.13 = (f32[1,1,4,64]{3,2,1,0:T(4,128)S(1)}, f32[1,1,4,64]{3,2,1,0:T(4,128)S(1)}, u32[]{:S(2)}, u32[]{:S(2)}) collective-permute-start(f32[1,1,4,64]{3,2,1,0:T(4,128)S(1)} %get-tuple-element.74), channel_id=1, source_target_pairs={{1,0},{2,1},{3,2},{4,3},{5,4},{6,5},{7,6},{0,7},{9,8},{10,9},{11,1... | collective-permute-start | bytes 3080 | tf_op jit(solution)/shard_map/ppermute | solution.py:19
  86.1 1.5 collective-permute-done.12
  87.7 9.6 %gather_fusion.3 = f32[1024]{0:T(1024)S(1)} fusion(f32[2,4,128]{2,1,0:T(4,128)S(1)} %fusion.57, s32[1024]{0:T(1024)S(1)} %bitcast.199), kind=kCustom, calls=%fused_computation.3.clone | custom fusion | bytes 20480 | tf_op jit(solution)/shard_map/jit(take_along_axis)/gather | solution.py:43
  97.4 1.7 collective-permute-start.19
  99.2 4.7 %collective-permute-start.17 = (f32[1,1,4,64]{3,2,1,0:T(4,128)S(1)}, f32[1,1,4,64]{3,2,1,0:T(4,128)S(1)}, u32[]{:S(2)}, u32[]{:S(2)}) collective-permute-start(f32[1,1,4,64]{3,2,1,0:T(4,128)S(1)} %get-tuple-element.70), channel_id=1, source_target_pairs={{1,0},{2,1},{3,2},{4,3},{5,4},{6,5},{7,6},{0,7},{9,8},{10,9},{11,1... | collective-permute-start | bytes 3080 | tf_op jit(solution)/shard_map/ppermute | solution.py:19
  104.0 1.5 collective-permute-done.16
  105.5 9.6 %gather_fusion.4 = f32[1024]{0:T(1024)S(1)} fusion(f32[2,4,128]{2,1,0:T(4,128)S(1)} %fusion.53, s32[1024]{0:T(1024)S(1)} %bitcast.200), kind=kCustom, calls=%fused_computation.4.clone | custom fusion | bytes 20480 | tf_op jit(solution)/shard_map/jit(take_along_axis)/gather | solution.py:43
  115.3 21.0 %all-gather.1 = f32[8,2,4]{2,1,0:T(2,128)S(1)} all-gather(f32[1,2,4]{2,1,0:T(2,128)S(1)} %bitcast.257), channel_id=1, replica_groups=mesh['srow'=4,'scol'=8] {'scol'}, dimensions={0}, use_global_device_ids=true | all-gather | bytes 288 | tf_op jit(solution)/shard_map/all_gather | solution.py:55
  136.8 1.7 collective-permute-start.23
  138.6 4.7 %collective-permute-start.21 = (f32[1,1,4,64]{3,2,1,0:T(4,128)S(1)}, f32[1,1,4,64]{3,2,1,0:T(4,128)S(1)}, u32[]{:S(2)}, u32[]{:S(2)}) collective-permute-start(f32[1,1,4,64]{3,2,1,0:T(4,128)S(1)} %get-tuple-element.66), channel_id=1, source_target_pairs={{1,0},{2,1},{3,2},{4,3},{5,4},{6,5},{7,6},{0,7},{9,8},{10,9},{11,1... | collective-permute-start | bytes 3080 | tf_op jit(solution)/shard_map/ppermute | solution.py:19
  143.4 1.5 collective-permute-done.20
  144.9 9.6 %gather_fusion.5 = f32[1024]{0:T(1024)S(1)} fusion(f32[2,4,128]{2,1,0:T(4,128)S(1)} %fusion.49, s32[1024]{0:T(1024)S(1)} %bitcast.201), kind=kCustom, calls=%fused_computation.5.clone | custom fusion | bytes 20480 | tf_op jit(solution)/shard_map/jit(take_along_axis)/gather | solution.py:43
  154.7 21.8 %all-reduce.2 = (f32[4]{0:T(128)S(1)}, f32[4]{0:T(128)S(1)}) all-reduce(f32[4]{0:T(128)S(1)} %get-tuple-element.8, f32[4]{0:T(128)S(1)} %get-tuple-element.7), channel_id=1, replica_groups=mesh['srow'=4,'scol'=8] {'scol'}, use_global_device_ids=true, to_apply=%region_1.3 | all-reduce | flops 8 | bytes 64 | tf_op jit(solution)/shard_map/psum | solution.py:68
  176.5 5.6 %all-reduce.5 = (f32[4]{0:T(128)S(1)}, f32[4]{0:T(128)S(1)}) all-reduce(f32[4]{0:T(128)S(1)} %get-tuple-element.13, f32[4]{0:T(128)S(1)} %get-tuple-element.14), channel_id=1, replica_groups=mesh['srow'=4,'scol'=8] {'srow'}, use_global_device_ids=true, to_apply=%region_2.4 | all-reduce | flops 8 | bytes 64 | tf_op jit(solution)/shard_map/psum | solution.py:68
  182.3 1.7 collective-permute-start.27
  184.1 4.7 %collective-permute-start.25 = (f32[1,1,4,64]{3,2,1,0:T(4,128)S(1)}, f32[1,1,4,64]{3,2,1,0:T(4,128)S(1)}, u32[]{:S(2)}, u32[]{:S(2)}) collective-permute-start(f32[1,1,4,64]{3,2,1,0:T(4,128)S(1)} %get-tuple-element.62), channel_id=1, source_target_pairs={{1,0},{2,1},{3,2},{4,3},{5,4},{6,5},{7,6},{0,7},{9,8},{10,9},{11,1... | collective-permute-start | bytes 3080 | tf_op jit(solution)/shard_map/ppermute | solution.py:19
  188.9 1.5 collective-permute-done.24
  190.5 9.6 %gather_fusion.6 = f32[1024]{0:T(1024)S(1)} fusion(f32[2,4,128]{2,1,0:T(4,128)S(1)} %fusion.45, s32[1024]{0:T(1024)S(1)} %bitcast.202), kind=kCustom, calls=%fused_computation.6.clone | custom fusion | bytes 20480 | tf_op jit(solution)/shard_map/jit(take_along_axis)/gather | solution.py:43
  200.5 1.8 collective-permute-start.31
  202.2 4.7 %collective-permute-start.29 = (f32[1,1,4,64]{3,2,1,0:T(4,128)S(1)}, f32[1,1,4,64]{3,2,1,0:T(4,128)S(1)}, u32[]{:S(2)}, u32[]{:S(2)}) collective-permute-start(f32[1,1,4,64]{3,2,1,0:T(4,128)S(1)} %get-tuple-element.58), channel_id=1, source_target_pairs={{1,0},{2,1},{3,2},{4,3},{5,4},{6,5},{7,6},{0,7},{9,8},{10,9},{11,1... | collective-permute-start | bytes 3080 | tf_op jit(solution)/shard_map/ppermute | solution.py:19
  207.0 1.5 collective-permute-done.28
  208.6 9.6 %gather_fusion.7 = f32[1024]{0:T(1024)S(1)} fusion(f32[2,4,128]{2,1,0:T(4,128)S(1)} %fusion.41, s32[1024]{0:T(1024)S(1)} %bitcast.203), kind=kCustom, calls=%fused_computation.7.clone | custom fusion | bytes 20480 | tf_op jit(solution)/shard_map/jit(take_along_axis)/gather | solution.py:43
  218.3 1.7 collective-permute-start.35
  220.0 4.7 %collective-permute-start.33 = (f32[1,1,4,64]{3,2,1,0:T(4,128)S(1)}, f32[1,1,4,64]{3,2,1,0:T(4,128)S(1)}, u32[]{:S(2)}, u32[]{:S(2)}) collective-permute-start(f32[1,1,4,64]{3,2,1,0:T(4,128)S(1)} %get-tuple-element.54), channel_id=1, source_target_pairs={{1,0},{2,1},{3,2},{4,3},{5,4},{6,5},{7,6},{0,7},{9,8},{10,9},{11,1... | collective-permute-start | bytes 3080 | tf_op jit(solution)/shard_map/ppermute | solution.py:19
  224.8 1.5 collective-permute-done.32
  226.4 9.6 %gather_fusion.8 = f32[1024]{0:T(1024)S(1)} fusion(f32[2,4,128]{2,1,0:T(4,128)S(1)} %fusion.37, s32[1024]{0:T(1024)S(1)} %bitcast.204), kind=kCustom, calls=%fused_computation.8.clone | custom fusion | bytes 20480 | tf_op jit(solution)/shard_map/jit(take_along_axis)/gather | solution.py:43
  236.2 21.0 %all-gather.2 = f32[8,2,4]{2,1,0:T(2,128)S(1)} all-gather(f32[1,2,4]{2,1,0:T(2,128)S(1)} %bitcast.258), channel_id=1, replica_groups=mesh['srow'=4,'scol'=8] {'scol'}, dimensions={0}, use_global_device_ids=true | all-gather | bytes 288 | tf_op jit(solution)/shard_map/all_gather | solution.py:55
  257.7 1.7 collective-permute-start.39
  259.4 4.7 %collective-permute-start.37 = (f32[1,1,4,64]{3,2,1,0:T(4,128)S(1)}, f32[1,1,4,64]{3,2,1,0:T(4,128)S(1)}, u32[]{:S(2)}, u32[]{:S(2)}) collective-permute-start(f32[1,1,4,64]{3,2,1,0:T(4,128)S(1)} %get-tuple-element.50), channel_id=1, source_target_pairs={{1,0},{2,1},{3,2},{4,3},{5,4},{6,5},{7,6},{0,7},{9,8},{10,9},{11,1... | collective-permute-start | bytes 3080 | tf_op jit(solution)/shard_map/ppermute | solution.py:19
  265.8 9.6 %gather_fusion.9 = f32[1024]{0:T(1024)S(1)} fusion(f32[2,4,128]{2,1,0:T(4,128)S(1)} %fusion.33, s32[1024]{0:T(1024)S(1)} %bitcast.205), kind=kCustom, calls=%fused_computation.9.clone | custom fusion | bytes 20480 | tf_op jit(solution)/shard_map/jit(take_along_axis)/gather | solution.py:43
  275.6 21.8 %all-reduce.1 = (f32[4]{0:T(128)S(1)}, f32[4]{0:T(128)S(1)}) all-reduce(f32[4]{0:T(128)S(1)} %get-tuple-element.6, f32[4]{0:T(128)S(1)} %get-tuple-element.5), channel_id=1, replica_groups=mesh['srow'=4,'scol'=8] {'scol'}, use_global_device_ids=true, to_apply=%region_7.9 | all-reduce | flops 8 | bytes 64 | tf_op jit(solution)/shard_map/psum | solution.py:68
  297.4 5.6 %all-reduce.4 = (f32[4]{0:T(128)S(1)}, f32[4]{0:T(128)S(1)}) all-reduce(f32[4]{0:T(128)S(1)} %get-tuple-element.11, f32[4]{0:T(128)S(1)} %get-tuple-element.12), channel_id=1, replica_groups=mesh['srow'=4,'scol'=8] {'srow'}, use_global_device_ids=true, to_apply=%region_8.10 | all-reduce | flops 8 | bytes 64 | tf_op jit(solution)/shard_map/psum | solution.py:68
  303.2 1.8 collective-permute-start.43
  305.0 4.7 %collective-permute-start.41 = (f32[1,1,4,64]{3,2,1,0:T(4,128)S(1)}, f32[1,1,4,64]{3,2,1,0:T(4,128)S(1)}, u32[]{:S(2)}, u32[]{:S(2)}) collective-permute-start(f32[1,1,4,64]{3,2,1,0:T(4,128)S(1)} %get-tuple-element.46), channel_id=1, source_target_pairs={{1,0},{2,1},{3,2},{4,3},{5,4},{6,5},{7,6},{0,7},{9,8},{10,9},{11,1... | collective-permute-start | bytes 3080 | tf_op jit(solution)/shard_map/ppermute | solution.py:19
  309.8 1.5 collective-permute-done.40
  311.4 9.6 %gather_fusion.10 = f32[1024]{0:T(1024)S(1)} fusion(f32[2,4,128]{2,1,0:T(4,128)S(1)} %fusion.29, s32[1024]{0:T(1024)S(1)} %bitcast.206), kind=kCustom, calls=%fused_computation.10.clone | custom fusion | bytes 20480 | tf_op jit(solution)/shard_map/jit(take_along_axis)/gather | solution.py:43
  321.4 1.8 collective-permute-start.47
  323.1 4.7 %collective-permute-start.45 = (f32[1,1,4,64]{3,2,1,0:T(4,128)S(1)}, f32[1,1,4,64]{3,2,1,0:T(4,128)S(1)}, u32[]{:S(2)}, u32[]{:S(2)}) collective-permute-start(f32[1,1,4,64]{3,2,1,0:T(4,128)S(1)} %get-tuple-element.42), channel_id=1, source_target_pairs={{1,0},{2,1},{3,2},{4,3},{5,4},{6,5},{7,6},{0,7},{9,8},{10,9},{11,1... | collective-permute-start | bytes 3080 | tf_op jit(solution)/shard_map/ppermute | solution.py:19
  327.9 1.5 collective-permute-done.44
  329.5 9.6 %gather_fusion.11 = f32[1024]{0:T(1024)S(1)} fusion(f32[2,4,128]{2,1,0:T(4,128)S(1)} %fusion.25, s32[1024]{0:T(1024)S(1)} %bitcast.207), kind=kCustom, calls=%fused_computation.11.clone | custom fusion | bytes 20480 | tf_op jit(solution)/shard_map/jit(take_along_axis)/gather | solution.py:43
  339.2 1.7 collective-permute-start.51
  340.9 4.7 %collective-permute-start.49 = (f32[1,1,4,64]{3,2,1,0:T(4,128)S(1)}, f32[1,1,4,64]{3,2,1,0:T(4,128)S(1)}, u32[]{:S(2)}, u32[]{:S(2)}) collective-permute-start(f32[1,1,4,64]{3,2,1,0:T(4,128)S(1)} %get-tuple-element.38), channel_id=1, source_target_pairs={{1,0},{2,1},{3,2},{4,3},{5,4},{6,5},{7,6},{0,7},{9,8},{10,9},{11,1... | collective-permute-start | bytes 3080 | tf_op jit(solution)/shard_map/ppermute | solution.py:19
  347.3 9.6 %gather_fusion.12 = f32[1024]{0:T(1024)S(1)} fusion(f32[2,4,128]{2,1,0:T(4,128)S(1)} %fusion.21, s32[1024]{0:T(1024)S(1)} %bitcast.208), kind=kCustom, calls=%fused_computation.12.clone | custom fusion | bytes 20480 | tf_op jit(solution)/shard_map/jit(take_along_axis)/gather | solution.py:43
  357.0 21.0 %all-gather.3 = f32[8,2,4]{2,1,0:T(2,128)S(1)} all-gather(f32[1,2,4]{2,1,0:T(2,128)S(1)} %bitcast.259), channel_id=1, replica_groups=mesh['srow'=4,'scol'=8] {'scol'}, dimensions={0}, use_global_device_ids=true | all-gather | bytes 288 | tf_op jit(solution)/shard_map/all_gather | solution.py:55
  378.6 1.7 collective-permute-start.55
  380.3 4.7 %collective-permute-start.53 = (f32[1,1,4,64]{3,2,1,0:T(4,128)S(1)}, f32[1,1,4,64]{3,2,1,0:T(4,128)S(1)}, u32[]{:S(2)}, u32[]{:S(2)}) collective-permute-start(f32[1,1,4,64]{3,2,1,0:T(4,128)S(1)} %get-tuple-element.34), channel_id=1, source_target_pairs={{1,0},{2,1},{3,2},{4,3},{5,4},{6,5},{7,6},{0,7},{9,8},{10,9},{11,1... | collective-permute-start | bytes 3080 | tf_op jit(solution)/shard_map/ppermute | solution.py:19
  385.1 1.5 collective-permute-done.52
  386.7 9.6 %gather_fusion.13 = f32[1024]{0:T(1024)S(1)} fusion(f32[2,4,128]{2,1,0:T(4,128)S(1)} %fusion.17, s32[1024]{0:T(1024)S(1)} %bitcast.209), kind=kCustom, calls=%fused_computation.13.clone | custom fusion | bytes 20480 | tf_op jit(solution)/shard_map/jit(take_along_axis)/gather | solution.py:43
  396.5 21.8 %all-reduce = (f32[4]{0:T(128)S(1)}, f32[4]{0:T(128)S(1)}) all-reduce(f32[4]{0:T(128)S(1)} %get-tuple-element.4, f32[4]{0:T(128)S(1)} %get-tuple-element.3), channel_id=1, replica_groups=mesh['srow'=4,'scol'=8] {'scol'}, use_global_device_ids=true, to_apply=%region_13.15 | all-reduce | flops 8 | bytes 64 | tf_op jit(solution)/shard_map/psum | solution.py:68
  418.3 5.6 %all-reduce.3 = (f32[4]{0:T(128)S(1)}, f32[4]{0:T(128)S(1)}) all-reduce(f32[4]{0:T(128)S(1)} %get-tuple-element.9, f32[4]{0:T(128)S(1)} %get-tuple-element.10), channel_id=1, replica_groups=mesh['srow'=4,'scol'=8] {'srow'}, use_global_device_ids=true, to_apply=%region_14.16 | all-reduce | flops 8 | bytes 64 | tf_op jit(solution)/shard_map/psum | solution.py:68
  (174 shorter events, 14.9 us)
Async XLA Ops:
  0.6 42.6 %copy-start = (f32[1,2,128,128]{3,2,1,0:T(8,128)S(1)}, f32[1,2,128,128]{3,2,1,0:T(8,128)}, u32[]{:S(2)}) copy-start(f32[1,2,128,128]{3,2,1,0:T(8,128)} %param.9) | copy-start | bytes 393220
  0.6 3.3 copy-start.2
  1.5 7.9 %collective-permute-start.2 = (f32[1,2,4,64]{3,2,1,0:T(4,128)S(1)}, f32[1,2,4,64]{3,2,1,0:T(4,128)S(1)}, u32[]{:S(2)}, u32[]{:S(2)}) collective-permute-start(f32[1,2,4,64]{3,2,1,0:T(4,128)S(1)} %get-tuple-element.83), channel_id=1, source_target_pairs={{0,8},{8,16},{16,24},{24,0},{1,9},{9,17},{17,25},{25,1},{2,10},{10... | collective-permute-start | bytes 6152 | tf_op jit(solution)/shard_map/ppermute | solution.py:17
  2.0 8.8 %collective-permute-start.3 = (f32[1,2,4,64]{3,2,1,0:T(4,128)S(1)}, f32[1,2,4,64]{3,2,1,0:T(4,128)S(1)}, u32[]{:S(2)}, u32[]{:S(2)}) collective-permute-start(f32[1,2,4,64]{3,2,1,0:T(4,128)S(1)} %get-tuple-element.83), channel_id=1, source_target_pairs={{8,0},{16,8},{24,16},{0,24},{9,1},{17,9},{25,17},{1,25},{10,2},{18... | collective-permute-start | bytes 6152 | tf_op jit(solution)/shard_map/ppermute | solution.py:19
  4.0 6.9 %collective-permute-start = (f32[1,1,4,64]{3,2,1,0:T(4,128)S(1)}, f32[1,1,4,64]{3,2,1,0:T(4,128)S(1)}, u32[]{:S(2)}, u32[]{:S(2)}) collective-permute-start(f32[1,1,4,64]{3,2,1,0:T(4,128)S(1)} %get-tuple-element.85), channel_id=1, source_target_pairs={{0,1},{1,2},{2,3},{3,4},{4,5},{5,6},{6,7},{7,0},{8,9},{9,10},{10,1... | collective-permute-start | bytes 3080 | tf_op jit(solution)/shard_map/ppermute | solution.py:17
  6.2 3.1 copy-start.5
  6.2 4.6 %collective-permute-start.1 = (f32[1,1,4,64]{3,2,1,0:T(4,128)S(1)}, f32[1,1,4,64]{3,2,1,0:T(4,128)S(1)}, u32[]{:S(2)}, u32[]{:S(2)}) collective-permute-start(f32[1,1,4,64]{3,2,1,0:T(4,128)S(1)} %get-tuple-element.86), channel_id=1, source_target_pairs={{1,0},{2,1},{3,2},{4,3},{5,4},{6,5},{7,6},{0,7},{9,8},{10,9},{11,1... | collective-permute-start | bytes 3080 | tf_op jit(solution)/shard_map/ppermute | solution.py:19
  20.5 0.7 copy-start.3
  42.4 0.7 copy-start.4
  43.6 6.5 %collective-permute-start.6 = (f32[1,2,4,64]{3,2,1,0:T(4,128)S(1)}, f32[1,2,4,64]{3,2,1,0:T(4,128)S(1)}, u32[]{:S(2)}, u32[]{:S(2)}) collective-permute-start(f32[1,2,4,64]{3,2,1,0:T(4,128)S(1)} %get-tuple-element.79), channel_id=1, source_target_pairs={{0,8},{8,16},{16,24},{24,0},{1,9},{9,17},{17,25},{25,1},{2,10},{10... | collective-permute-start | bytes 6152 | tf_op jit(solution)/shard_map/ppermute | solution.py:17
  43.6 8.0 %collective-permute-start.7 = (f32[1,2,4,64]{3,2,1,0:T(4,128)S(1)}, f32[1,2,4,64]{3,2,1,0:T(4,128)S(1)}, u32[]{:S(2)}, u32[]{:S(2)}) collective-permute-start(f32[1,2,4,64]{3,2,1,0:T(4,128)S(1)} %get-tuple-element.79), channel_id=1, source_target_pairs={{8,0},{16,8},{24,16},{0,24},{9,1},{17,9},{25,17},{1,25},{10,2},{18... | collective-permute-start | bytes 6152 | tf_op jit(solution)/shard_map/ppermute | solution.py:19
  45.4 6.3 %collective-permute-start.4 = (f32[1,1,4,64]{3,2,1,0:T(4,128)S(1)}, f32[1,1,4,64]{3,2,1,0:T(4,128)S(1)}, u32[]{:S(2)}, u32[]{:S(2)}) collective-permute-start(f32[1,1,4,64]{3,2,1,0:T(4,128)S(1)} %get-tuple-element.81), channel_id=1, source_target_pairs={{0,1},{1,2},{2,3},{3,4},{4,5},{5,6},{6,7},{7,0},{8,9},{9,10},{10,1... | collective-permute-start | bytes 3080 | tf_op jit(solution)/shard_map/ppermute | solution.py:17
  45.4 6.3 %collective-permute-start.5 = (f32[1,1,4,64]{3,2,1,0:T(4,128)S(1)}, f32[1,1,4,64]{3,2,1,0:T(4,128)S(1)}, u32[]{:S(2)}, u32[]{:S(2)}) collective-permute-start(f32[1,1,4,64]{3,2,1,0:T(4,128)S(1)} %get-tuple-element.82), channel_id=1, source_target_pairs={{1,0},{2,1},{3,2},{4,3},{5,4},{6,5},{7,6},{0,7},{9,8},{10,9},{11,1... | collective-permute-start | bytes 3080 | tf_op jit(solution)/shard_map/ppermute | solution.py:19
  61.4 6.5 %collective-permute-start.10 = (f32[1,2,4,64]{3,2,1,0:T(4,128)S(1)}, f32[1,2,4,64]{3,2,1,0:T(4,128)S(1)}, u32[]{:S(2)}, u32[]{:S(2)}) collective-permute-start(f32[1,2,4,64]{3,2,1,0:T(4,128)S(1)} %get-tuple-element.75), channel_id=1, source_target_pairs={{0,8},{8,16},{16,24},{24,0},{1,9},{9,17},{17,25},{25,1},{2,10},{10... | collective-permute-start | bytes 6152 | tf_op jit(solution)/shard_map/ppermute | solution.py:17
  61.5 8.0 %collective-permute-start.11 = (f32[1,2,4,64]{3,2,1,0:T(4,128)S(1)}, f32[1,2,4,64]{3,2,1,0:T(4,128)S(1)}, u32[]{:S(2)}, u32[]{:S(2)}) collective-permute-start(f32[1,2,4,64]{3,2,1,0:T(4,128)S(1)} %get-tuple-element.75), channel_id=1, source_target_pairs={{8,0},{16,8},{24,16},{0,24},{9,1},{17,9},{25,17},{1,25},{10,2},{18... | collective-permute-start | bytes 6152 | tf_op jit(solution)/shard_map/ppermute | solution.py:19
  63.2 6.3 %collective-permute-start.8 = (f32[1,1,4,64]{3,2,1,0:T(4,128)S(1)}, f32[1,1,4,64]{3,2,1,0:T(4,128)S(1)}, u32[]{:S(2)}, u32[]{:S(2)}) collective-permute-start(f32[1,1,4,64]{3,2,1,0:T(4,128)S(1)} %get-tuple-element.77), channel_id=1, source_target_pairs={{0,1},{1,2},{2,3},{3,4},{4,5},{5,6},{6,7},{7,0},{8,9},{9,10},{10,1... | collective-permute-start | bytes 3080 | tf_op jit(solution)/shard_map/ppermute | solution.py:17
  63.2 6.3 %collective-permute-start.9 = (f32[1,1,4,64]{3,2,1,0:T(4,128)S(1)}, f32[1,1,4,64]{3,2,1,0:T(4,128)S(1)}, u32[]{:S(2)}, u32[]{:S(2)}) collective-permute-start(f32[1,1,4,64]{3,2,1,0:T(4,128)S(1)} %get-tuple-element.78), channel_id=1, source_target_pairs={{1,0},{2,1},{3,2},{4,3},{5,4},{6,5},{7,6},{0,7},{9,8},{10,9},{11,1... | collective-permute-start | bytes 3080 | tf_op jit(solution)/shard_map/ppermute | solution.py:19
  69.6 9.6 %copy-start.1 = (f32[1,2,128,128]{3,2,1,0:T(8,128)S(1)}, f32[1,2,128,128]{3,2,1,0:T(8,128)}, u32[]{:S(2)}) copy-start(f32[1,2,128,128]{3,2,1,0:T(8,128)} %param.10) | copy-start | bytes 393220
  79.6 6.5 %collective-permute-start.14 = (f32[1,2,4,64]{3,2,1,0:T(4,128)S(1)}, f32[1,2,4,64]{3,2,1,0:T(4,128)S(1)}, u32[]{:S(2)}, u32[]{:S(2)}) collective-permute-start(f32[1,2,4,64]{3,2,1,0:T(4,128)S(1)} %get-tuple-element.71), channel_id=1, source_target_pairs={{0,8},{8,16},{16,24},{24,0},{1,9},{9,17},{17,25},{25,1},{2,10},{10... | collective-permute-start | bytes 6152 | tf_op jit(solution)/shard_map/ppermute | solution.py:17
  79.6 8.0 %collective-permute-start.15 = (f32[1,2,4,64]{3,2,1,0:T(4,128)S(1)}, f32[1,2,4,64]{3,2,1,0:T(4,128)S(1)}, u32[]{:S(2)}, u32[]{:S(2)}) collective-permute-start(f32[1,2,4,64]{3,2,1,0:T(4,128)S(1)} %get-tuple-element.71), channel_id=1, source_target_pairs={{8,0},{16,8},{24,16},{0,24},{9,1},{17,9},{25,17},{1,25},{10,2},{18... | collective-permute-start | bytes 6152 | tf_op jit(solution)/shard_map/ppermute | solution.py:19
  81.3 6.3 %collective-permute-start.12 = (f32[1,1,4,64]{3,2,1,0:T(4,128)S(1)}, f32[1,1,4,64]{3,2,1,0:T(4,128)S(1)}, u32[]{:S(2)}, u32[]{:S(2)}) collective-permute-start(f32[1,1,4,64]{3,2,1,0:T(4,128)S(1)} %get-tuple-element.73), channel_id=1, source_target_pairs={{0,1},{1,2},{2,3},{3,4},{4,5},{5,6},{6,7},{7,0},{8,9},{9,10},{10,1... | collective-permute-start | bytes 3080 | tf_op jit(solution)/shard_map/ppermute | solution.py:17
  81.3 6.3 %collective-permute-start.13 = (f32[1,1,4,64]{3,2,1,0:T(4,128)S(1)}, f32[1,1,4,64]{3,2,1,0:T(4,128)S(1)}, u32[]{:S(2)}, u32[]{:S(2)}) collective-permute-start(f32[1,1,4,64]{3,2,1,0:T(4,128)S(1)} %get-tuple-element.74), channel_id=1, source_target_pairs={{1,0},{2,1},{3,2},{4,3},{5,4},{6,5},{7,6},{0,7},{9,8},{10,9},{11,1... | collective-permute-start | bytes 3080 | tf_op jit(solution)/shard_map/ppermute | solution.py:19
  97.4 6.5 %collective-permute-start.18 = (f32[1,2,4,64]{3,2,1,0:T(4,128)S(1)}, f32[1,2,4,64]{3,2,1,0:T(4,128)S(1)}, u32[]{:S(2)}, u32[]{:S(2)}) collective-permute-start(f32[1,2,4,64]{3,2,1,0:T(4,128)S(1)} %get-tuple-element.67), channel_id=1, source_target_pairs={{0,8},{8,16},{16,24},{24,0},{1,9},{9,17},{17,25},{25,1},{2,10},{10... | collective-permute-start | bytes 6152 | tf_op jit(solution)/shard_map/ppermute | solution.py:17
  97.4 8.0 %collective-permute-start.19 = (f32[1,2,4,64]{3,2,1,0:T(4,128)S(1)}, f32[1,2,4,64]{3,2,1,0:T(4,128)S(1)}, u32[]{:S(2)}, u32[]{:S(2)}) collective-permute-start(f32[1,2,4,64]{3,2,1,0:T(4,128)S(1)} %get-tuple-element.67), channel_id=1, source_target_pairs={{8,0},{16,8},{24,16},{0,24},{9,1},{17,9},{25,17},{1,25},{10,2},{18... | collective-permute-start | bytes 6152 | tf_op jit(solution)/shard_map/ppermute | solution.py:19
  99.2 6.3 %collective-permute-start.16 = (f32[1,1,4,64]{3,2,1,0:T(4,128)S(1)}, f32[1,1,4,64]{3,2,1,0:T(4,128)S(1)}, u32[]{:S(2)}, u32[]{:S(2)}) collective-permute-start(f32[1,1,4,64]{3,2,1,0:T(4,128)S(1)} %get-tuple-element.69), channel_id=1, source_target_pairs={{0,1},{1,2},{2,3},{3,4},{4,5},{5,6},{6,7},{7,0},{8,9},{9,10},{10,1... | collective-permute-start | bytes 3080 | tf_op jit(solution)/shard_map/ppermute | solution.py:17
  99.2 6.3 %collective-permute-start.17 = (f32[1,1,4,64]{3,2,1,0:T(4,128)S(1)}, f32[1,1,4,64]{3,2,1,0:T(4,128)S(1)}, u32[]{:S(2)}, u32[]{:S(2)}) collective-permute-start(f32[1,1,4,64]{3,2,1,0:T(4,128)S(1)} %get-tuple-element.70), channel_id=1, source_target_pairs={{1,0},{2,1},{3,2},{4,3},{5,4},{6,5},{7,6},{0,7},{9,8},{10,9},{11,1... | collective-permute-start | bytes 3080 | tf_op jit(solution)/shard_map/ppermute | solution.py:19
  136.8 6.5 %collective-permute-start.22 = (f32[1,2,4,64]{3,2,1,0:T(4,128)S(1)}, f32[1,2,4,64]{3,2,1,0:T(4,128)S(1)}, u32[]{:S(2)}, u32[]{:S(2)}) collective-permute-start(f32[1,2,4,64]{3,2,1,0:T(4,128)S(1)} %get-tuple-element.63), channel_id=1, source_target_pairs={{0,8},{8,16},{16,24},{24,0},{1,9},{9,17},{17,25},{25,1},{2,10},{10... | collective-permute-start | bytes 6152 | tf_op jit(solution)/shard_map/ppermute | solution.py:17
  136.8 8.0 %collective-permute-start.23 = (f32[1,2,4,64]{3,2,1,0:T(4,128)S(1)}, f32[1,2,4,64]{3,2,1,0:T(4,128)S(1)}, u32[]{:S(2)}, u32[]{:S(2)}) collective-permute-start(f32[1,2,4,64]{3,2,1,0:T(4,128)S(1)} %get-tuple-element.63), channel_id=1, source_target_pairs={{8,0},{16,8},{24,16},{0,24},{9,1},{17,9},{25,17},{1,25},{10,2},{18... | collective-permute-start | bytes 6152 | tf_op jit(solution)/shard_map/ppermute | solution.py:19
  138.6 6.3 %collective-permute-start.20 = (f32[1,1,4,64]{3,2,1,0:T(4,128)S(1)}, f32[1,1,4,64]{3,2,1,0:T(4,128)S(1)}, u32[]{:S(2)}, u32[]{:S(2)}) collective-permute-start(f32[1,1,4,64]{3,2,1,0:T(4,128)S(1)} %get-tuple-element.65), channel_id=1, source_target_pairs={{0,1},{1,2},{2,3},{3,4},{4,5},{5,6},{6,7},{7,0},{8,9},{9,10},{10,1... | collective-permute-start | bytes 3080 | tf_op jit(solution)/shard_map/ppermute | solution.py:17
  138.6 6.3 %collective-permute-start.21 = (f32[1,1,4,64]{3,2,1,0:T(4,128)S(1)}, f32[1,1,4,64]{3,2,1,0:T(4,128)S(1)}, u32[]{:S(2)}, u32[]{:S(2)}) collective-permute-start(f32[1,1,4,64]{3,2,1,0:T(4,128)S(1)} %get-tuple-element.66), channel_id=1, source_target_pairs={{1,0},{2,1},{3,2},{4,3},{5,4},{6,5},{7,6},{0,7},{9,8},{10,9},{11,1... | collective-permute-start | bytes 3080 | tf_op jit(solution)/shard_map/ppermute | solution.py:19
  182.3 6.5 %collective-permute-start.26 = (f32[1,2,4,64]{3,2,1,0:T(4,128)S(1)}, f32[1,2,4,64]{3,2,1,0:T(4,128)S(1)}, u32[]{:S(2)}, u32[]{:S(2)}) collective-permute-start(f32[1,2,4,64]{3,2,1,0:T(4,128)S(1)} %get-tuple-element.59), channel_id=1, source_target_pairs={{0,8},{8,16},{16,24},{24,0},{1,9},{9,17},{17,25},{25,1},{2,10},{10... | collective-permute-start | bytes 6152 | tf_op jit(solution)/shard_map/ppermute | solution.py:17
  182.3 8.0 %collective-permute-start.27 = (f32[1,2,4,64]{3,2,1,0:T(4,128)S(1)}, f32[1,2,4,64]{3,2,1,0:T(4,128)S(1)}, u32[]{:S(2)}, u32[]{:S(2)}) collective-permute-start(f32[1,2,4,64]{3,2,1,0:T(4,128)S(1)} %get-tuple-element.59), channel_id=1, source_target_pairs={{8,0},{16,8},{24,16},{0,24},{9,1},{17,9},{25,17},{1,25},{10,2},{18... | collective-permute-start | bytes 6152 | tf_op jit(solution)/shard_map/ppermute | solution.py:19
  184.1 6.3 %collective-permute-start.24 = (f32[1,1,4,64]{3,2,1,0:T(4,128)S(1)}, f32[1,1,4,64]{3,2,1,0:T(4,128)S(1)}, u32[]{:S(2)}, u32[]{:S(2)}) collective-permute-start(f32[1,1,4,64]{3,2,1,0:T(4,128)S(1)} %get-tuple-element.61), channel_id=1, source_target_pairs={{0,1},{1,2},{2,3},{3,4},{4,5},{5,6},{6,7},{7,0},{8,9},{9,10},{10,1... | collective-permute-start | bytes 3080 | tf_op jit(solution)/shard_map/ppermute | solution.py:17
  184.1 6.3 %collective-permute-start.25 = (f32[1,1,4,64]{3,2,1,0:T(4,128)S(1)}, f32[1,1,4,64]{3,2,1,0:T(4,128)S(1)}, u32[]{:S(2)}, u32[]{:S(2)}) collective-permute-start(f32[1,1,4,64]{3,2,1,0:T(4,128)S(1)} %get-tuple-element.62), channel_id=1, source_target_pairs={{1,0},{2,1},{3,2},{4,3},{5,4},{6,5},{7,6},{0,7},{9,8},{10,9},{11,1... | collective-permute-start | bytes 3080 | tf_op jit(solution)/shard_map/ppermute | solution.py:19
  200.5 6.5 %collective-permute-start.30 = (f32[1,2,4,64]{3,2,1,0:T(4,128)S(1)}, f32[1,2,4,64]{3,2,1,0:T(4,128)S(1)}, u32[]{:S(2)}, u32[]{:S(2)}) collective-permute-start(f32[1,2,4,64]{3,2,1,0:T(4,128)S(1)} %get-tuple-element.55), channel_id=1, source_target_pairs={{0,8},{8,16},{16,24},{24,0},{1,9},{9,17},{17,25},{25,1},{2,10},{10... | collective-permute-start | bytes 6152 | tf_op jit(solution)/shard_map/ppermute | solution.py:17
  200.5 8.0 %collective-permute-start.31 = (f32[1,2,4,64]{3,2,1,0:T(4,128)S(1)}, f32[1,2,4,64]{3,2,1,0:T(4,128)S(1)}, u32[]{:S(2)}, u32[]{:S(2)}) collective-permute-start(f32[1,2,4,64]{3,2,1,0:T(4,128)S(1)} %get-tuple-element.55), channel_id=1, source_target_pairs={{8,0},{16,8},{24,16},{0,24},{9,1},{17,9},{25,17},{1,25},{10,2},{18... | collective-permute-start | bytes 6152 | tf_op jit(solution)/shard_map/ppermute | solution.py:19
  202.2 6.3 %collective-permute-start.28 = (f32[1,1,4,64]{3,2,1,0:T(4,128)S(1)}, f32[1,1,4,64]{3,2,1,0:T(4,128)S(1)}, u32[]{:S(2)}, u32[]{:S(2)}) collective-permute-start(f32[1,1,4,64]{3,2,1,0:T(4,128)S(1)} %get-tuple-element.57), channel_id=1, source_target_pairs={{0,1},{1,2},{2,3},{3,4},{4,5},{5,6},{6,7},{7,0},{8,9},{9,10},{10,1... | collective-permute-start | bytes 3080 | tf_op jit(solution)/shard_map/ppermute | solution.py:17
  202.2 6.3 %collective-permute-start.29 = (f32[1,1,4,64]{3,2,1,0:T(4,128)S(1)}, f32[1,1,4,64]{3,2,1,0:T(4,128)S(1)}, u32[]{:S(2)}, u32[]{:S(2)}) collective-permute-start(f32[1,1,4,64]{3,2,1,0:T(4,128)S(1)} %get-tuple-element.58), channel_id=1, source_target_pairs={{1,0},{2,1},{3,2},{4,3},{5,4},{6,5},{7,6},{0,7},{9,8},{10,9},{11,1... | collective-permute-start | bytes 3080 | tf_op jit(solution)/shard_map/ppermute | solution.py:19
  218.3 6.5 %collective-permute-start.34 = (f32[1,2,4,64]{3,2,1,0:T(4,128)S(1)}, f32[1,2,4,64]{3,2,1,0:T(4,128)S(1)}, u32[]{:S(2)}, u32[]{:S(2)}) collective-permute-start(f32[1,2,4,64]{3,2,1,0:T(4,128)S(1)} %get-tuple-element.51), channel_id=1, source_target_pairs={{0,8},{8,16},{16,24},{24,0},{1,9},{9,17},{17,25},{25,1},{2,10},{10... | collective-permute-start | bytes 6152 | tf_op jit(solution)/shard_map/ppermute | solution.py:17
  218.3 8.0 %collective-permute-start.35 = (f32[1,2,4,64]{3,2,1,0:T(4,128)S(1)}, f32[1,2,4,64]{3,2,1,0:T(4,128)S(1)}, u32[]{:S(2)}, u32[]{:S(2)}) collective-permute-start(f32[1,2,4,64]{3,2,1,0:T(4,128)S(1)} %get-tuple-element.51), channel_id=1, source_target_pairs={{8,0},{16,8},{24,16},{0,24},{9,1},{17,9},{25,17},{1,25},{10,2},{18... | collective-permute-start | bytes 6152 | tf_op jit(solution)/shard_map/ppermute | solution.py:19
  220.0 6.3 %collective-permute-start.32 = (f32[1,1,4,64]{3,2,1,0:T(4,128)S(1)}, f32[1,1,4,64]{3,2,1,0:T(4,128)S(1)}, u32[]{:S(2)}, u32[]{:S(2)}) collective-permute-start(f32[1,1,4,64]{3,2,1,0:T(4,128)S(1)} %get-tuple-element.53), channel_id=1, source_target_pairs={{0,1},{1,2},{2,3},{3,4},{4,5},{5,6},{6,7},{7,0},{8,9},{9,10},{10,1... | collective-permute-start | bytes 3080 | tf_op jit(solution)/shard_map/ppermute | solution.py:17
  220.0 6.3 %collective-permute-start.33 = (f32[1,1,4,64]{3,2,1,0:T(4,128)S(1)}, f32[1,1,4,64]{3,2,1,0:T(4,128)S(1)}, u32[]{:S(2)}, u32[]{:S(2)}) collective-permute-start(f32[1,1,4,64]{3,2,1,0:T(4,128)S(1)} %get-tuple-element.54), channel_id=1, source_target_pairs={{1,0},{2,1},{3,2},{4,3},{5,4},{6,5},{7,6},{0,7},{9,8},{10,9},{11,1... | collective-permute-start | bytes 3080 | tf_op jit(solution)/shard_map/ppermute | solution.py:19
  257.7 6.5 %collective-permute-start.38 = (f32[1,2,4,64]{3,2,1,0:T(4,128)S(1)}, f32[1,2,4,64]{3,2,1,0:T(4,128)S(1)}, u32[]{:S(2)}, u32[]{:S(2)}) collective-permute-start(f32[1,2,4,64]{3,2,1,0:T(4,128)S(1)} %get-tuple-element.47), channel_id=1, source_target_pairs={{0,8},{8,16},{16,24},{24,0},{1,9},{9,17},{17,25},{25,1},{2,10},{10... | collective-permute-start | bytes 6152 | tf_op jit(solution)/shard_map/ppermute | solution.py:17
  257.7 8.0 %collective-permute-start.39 = (f32[1,2,4,64]{3,2,1,0:T(4,128)S(1)}, f32[1,2,4,64]{3,2,1,0:T(4,128)S(1)}, u32[]{:S(2)}, u32[]{:S(2)}) collective-permute-start(f32[1,2,4,64]{3,2,1,0:T(4,128)S(1)} %get-tuple-element.47), channel_id=1, source_target_pairs={{8,0},{16,8},{24,16},{0,24},{9,1},{17,9},{25,17},{1,25},{10,2},{18... | collective-permute-start | bytes 6152 | tf_op jit(solution)/shard_map/ppermute | solution.py:19
  259.4 6.3 %collective-permute-start.36 = (f32[1,1,4,64]{3,2,1,0:T(4,128)S(1)}, f32[1,1,4,64]{3,2,1,0:T(4,128)S(1)}, u32[]{:S(2)}, u32[]{:S(2)}) collective-permute-start(f32[1,1,4,64]{3,2,1,0:T(4,128)S(1)} %get-tuple-element.49), channel_id=1, source_target_pairs={{0,1},{1,2},{2,3},{3,4},{4,5},{5,6},{6,7},{7,0},{8,9},{9,10},{10,1... | collective-permute-start | bytes 3080 | tf_op jit(solution)/shard_map/ppermute | solution.py:17
  259.4 6.3 %collective-permute-start.37 = (f32[1,1,4,64]{3,2,1,0:T(4,128)S(1)}, f32[1,1,4,64]{3,2,1,0:T(4,128)S(1)}, u32[]{:S(2)}, u32[]{:S(2)}) collective-permute-start(f32[1,1,4,64]{3,2,1,0:T(4,128)S(1)} %get-tuple-element.50), channel_id=1, source_target_pairs={{1,0},{2,1},{3,2},{4,3},{5,4},{6,5},{7,6},{0,7},{9,8},{10,9},{11,1... | collective-permute-start | bytes 3080 | tf_op jit(solution)/shard_map/ppermute | solution.py:19
  303.2 6.5 %collective-permute-start.42 = (f32[1,2,4,64]{3,2,1,0:T(4,128)S(1)}, f32[1,2,4,64]{3,2,1,0:T(4,128)S(1)}, u32[]{:S(2)}, u32[]{:S(2)}) collective-permute-start(f32[1,2,4,64]{3,2,1,0:T(4,128)S(1)} %get-tuple-element.43), channel_id=1, source_target_pairs={{0,8},{8,16},{16,24},{24,0},{1,9},{9,17},{17,25},{25,1},{2,10},{10... | collective-permute-start | bytes 6152 | tf_op jit(solution)/shard_map/ppermute | solution.py:17
  303.2 8.0 %collective-permute-start.43 = (f32[1,2,4,64]{3,2,1,0:T(4,128)S(1)}, f32[1,2,4,64]{3,2,1,0:T(4,128)S(1)}, u32[]{:S(2)}, u32[]{:S(2)}) collective-permute-start(f32[1,2,4,64]{3,2,1,0:T(4,128)S(1)} %get-tuple-element.43), channel_id=1, source_target_pairs={{8,0},{16,8},{24,16},{0,24},{9,1},{17,9},{25,17},{1,25},{10,2},{18... | collective-permute-start | bytes 6152 | tf_op jit(solution)/shard_map/ppermute | solution.py:19
  305.0 6.3 %collective-permute-start.40 = (f32[1,1,4,64]{3,2,1,0:T(4,128)S(1)}, f32[1,1,4,64]{3,2,1,0:T(4,128)S(1)}, u32[]{:S(2)}, u32[]{:S(2)}) collective-permute-start(f32[1,1,4,64]{3,2,1,0:T(4,128)S(1)} %get-tuple-element.45), channel_id=1, source_target_pairs={{0,1},{1,2},{2,3},{3,4},{4,5},{5,6},{6,7},{7,0},{8,9},{9,10},{10,1... | collective-permute-start | bytes 3080 | tf_op jit(solution)/shard_map/ppermute | solution.py:17
  305.0 6.3 %collective-permute-start.41 = (f32[1,1,4,64]{3,2,1,0:T(4,128)S(1)}, f32[1,1,4,64]{3,2,1,0:T(4,128)S(1)}, u32[]{:S(2)}, u32[]{:S(2)}) collective-permute-start(f32[1,1,4,64]{3,2,1,0:T(4,128)S(1)} %get-tuple-element.46), channel_id=1, source_target_pairs={{1,0},{2,1},{3,2},{4,3},{5,4},{6,5},{7,6},{0,7},{9,8},{10,9},{11,1... | collective-permute-start | bytes 3080 | tf_op jit(solution)/shard_map/ppermute | solution.py:19
  321.3 6.5 %collective-permute-start.46 = (f32[1,2,4,64]{3,2,1,0:T(4,128)S(1)}, f32[1,2,4,64]{3,2,1,0:T(4,128)S(1)}, u32[]{:S(2)}, u32[]{:S(2)}) collective-permute-start(f32[1,2,4,64]{3,2,1,0:T(4,128)S(1)} %get-tuple-element.39), channel_id=1, source_target_pairs={{0,8},{8,16},{16,24},{24,0},{1,9},{9,17},{17,25},{25,1},{2,10},{10... | collective-permute-start | bytes 6152 | tf_op jit(solution)/shard_map/ppermute | solution.py:17
  321.4 8.0 %collective-permute-start.47 = (f32[1,2,4,64]{3,2,1,0:T(4,128)S(1)}, f32[1,2,4,64]{3,2,1,0:T(4,128)S(1)}, u32[]{:S(2)}, u32[]{:S(2)}) collective-permute-start(f32[1,2,4,64]{3,2,1,0:T(4,128)S(1)} %get-tuple-element.39), channel_id=1, source_target_pairs={{8,0},{16,8},{24,16},{0,24},{9,1},{17,9},{25,17},{1,25},{10,2},{18... | collective-permute-start | bytes 6152 | tf_op jit(solution)/shard_map/ppermute | solution.py:19
  323.1 6.3 %collective-permute-start.44 = (f32[1,1,4,64]{3,2,1,0:T(4,128)S(1)}, f32[1,1,4,64]{3,2,1,0:T(4,128)S(1)}, u32[]{:S(2)}, u32[]{:S(2)}) collective-permute-start(f32[1,1,4,64]{3,2,1,0:T(4,128)S(1)} %get-tuple-element.41), channel_id=1, source_target_pairs={{0,1},{1,2},{2,3},{3,4},{4,5},{5,6},{6,7},{7,0},{8,9},{9,10},{10,1... | collective-permute-start | bytes 3080 | tf_op jit(solution)/shard_map/ppermute | solution.py:17
  323.1 6.3 %collective-permute-start.45 = (f32[1,1,4,64]{3,2,1,0:T(4,128)S(1)}, f32[1,1,4,64]{3,2,1,0:T(4,128)S(1)}, u32[]{:S(2)}, u32[]{:S(2)}) collective-permute-start(f32[1,1,4,64]{3,2,1,0:T(4,128)S(1)} %get-tuple-element.42), channel_id=1, source_target_pairs={{1,0},{2,1},{3,2},{4,3},{5,4},{6,5},{7,6},{0,7},{9,8},{10,9},{11,1... | collective-permute-start | bytes 3080 | tf_op jit(solution)/shard_map/ppermute | solution.py:19
  339.2 6.5 %collective-permute-start.50 = (f32[1,2,4,64]{3,2,1,0:T(4,128)S(1)}, f32[1,2,4,64]{3,2,1,0:T(4,128)S(1)}, u32[]{:S(2)}, u32[]{:S(2)}) collective-permute-start(f32[1,2,4,64]{3,2,1,0:T(4,128)S(1)} %get-tuple-element.35), channel_id=1, source_target_pairs={{0,8},{8,16},{16,24},{24,0},{1,9},{9,17},{17,25},{25,1},{2,10},{10... | collective-permute-start | bytes 6152 | tf_op jit(solution)/shard_map/ppermute | solution.py:17
  339.2 8.0 %collective-permute-start.51 = (f32[1,2,4,64]{3,2,1,0:T(4,128)S(1)}, f32[1,2,4,64]{3,2,1,0:T(4,128)S(1)}, u32[]{:S(2)}, u32[]{:S(2)}) collective-permute-start(f32[1,2,4,64]{3,2,1,0:T(4,128)S(1)} %get-tuple-element.35), channel_id=1, source_target_pairs={{8,0},{16,8},{24,16},{0,24},{9,1},{17,9},{25,17},{1,25},{10,2},{18... | collective-permute-start | bytes 6152 | tf_op jit(solution)/shard_map/ppermute | solution.py:19
  340.9 6.3 %collective-permute-start.48 = (f32[1,1,4,64]{3,2,1,0:T(4,128)S(1)}, f32[1,1,4,64]{3,2,1,0:T(4,128)S(1)}, u32[]{:S(2)}, u32[]{:S(2)}) collective-permute-start(f32[1,1,4,64]{3,2,1,0:T(4,128)S(1)} %get-tuple-element.37), channel_id=1, source_target_pairs={{0,1},{1,2},{2,3},{3,4},{4,5},{5,6},{6,7},{7,0},{8,9},{9,10},{10,1... | collective-permute-start | bytes 3080 | tf_op jit(solution)/shard_map/ppermute | solution.py:17
  340.9 6.3 %collective-permute-start.49 = (f32[1,1,4,64]{3,2,1,0:T(4,128)S(1)}, f32[1,1,4,64]{3,2,1,0:T(4,128)S(1)}, u32[]{:S(2)}, u32[]{:S(2)}) collective-permute-start(f32[1,1,4,64]{3,2,1,0:T(4,128)S(1)} %get-tuple-element.38), channel_id=1, source_target_pairs={{1,0},{2,1},{3,2},{4,3},{5,4},{6,5},{7,6},{0,7},{9,8},{10,9},{11,1... | collective-permute-start | bytes 3080 | tf_op jit(solution)/shard_map/ppermute | solution.py:19
  378.6 6.5 %collective-permute-start.54 = (f32[1,2,4,64]{3,2,1,0:T(4,128)S(1)}, f32[1,2,4,64]{3,2,1,0:T(4,128)S(1)}, u32[]{:S(2)}, u32[]{:S(2)}) collective-permute-start(f32[1,2,4,64]{3,2,1,0:T(4,128)S(1)} %get-tuple-element.31), channel_id=1, source_target_pairs={{0,8},{8,16},{16,24},{24,0},{1,9},{9,17},{17,25},{25,1},{2,10},{10... | collective-permute-start | bytes 6152 | tf_op jit(solution)/shard_map/ppermute | solution.py:17
  378.6 8.0 %collective-permute-start.55 = (f32[1,2,4,64]{3,2,1,0:T(4,128)S(1)}, f32[1,2,4,64]{3,2,1,0:T(4,128)S(1)}, u32[]{:S(2)}, u32[]{:S(2)}) collective-permute-start(f32[1,2,4,64]{3,2,1,0:T(4,128)S(1)} %get-tuple-element.31), channel_id=1, source_target_pairs={{8,0},{16,8},{24,16},{0,24},{9,1},{17,9},{25,17},{1,25},{10,2},{18... | collective-permute-start | bytes 6152 | tf_op jit(solution)/shard_map/ppermute | solution.py:19
  380.3 6.3 %collective-permute-start.52 = (f32[1,1,4,64]{3,2,1,0:T(4,128)S(1)}, f32[1,1,4,64]{3,2,1,0:T(4,128)S(1)}, u32[]{:S(2)}, u32[]{:S(2)}) collective-permute-start(f32[1,1,4,64]{3,2,1,0:T(4,128)S(1)} %get-tuple-element.33), channel_id=1, source_target_pairs={{0,1},{1,2},{2,3},{3,4},{4,5},{5,6},{6,7},{7,0},{8,9},{9,10},{10,1... | collective-permute-start | bytes 3080 | tf_op jit(solution)/shard_map/ppermute | solution.py:17
  380.3 6.3 %collective-permute-start.53 = (f32[1,1,4,64]{3,2,1,0:T(4,128)S(1)}, f32[1,1,4,64]{3,2,1,0:T(4,128)S(1)}, u32[]{:S(2)}, u32[]{:S(2)}) collective-permute-start(f32[1,1,4,64]{3,2,1,0:T(4,128)S(1)} %get-tuple-element.34), channel_id=1, source_target_pairs={{1,0},{2,1},{3,2},{4,3},{5,4},{6,5},{7,6},{0,7},{9,8},{10,9},{11,1... | collective-permute-start | bytes 3080 | tf_op jit(solution)/shard_map/ppermute | solution.py:19
